TPU v7x, 8 devices: a whole 2x2x1 slice. The times are simulated.
8 devices in a mesh: dp: 2 (over z, y), ep: 4 (over x, core).
Axes of the slice: x: 2, y: 2, z: 1, core: 2. Of those that a mesh axis runs over, the one named last changes fastest.
Arguments:
- hidden: bfloat16 [16384, 1024], P(('dp', 'ep'))
- grad_out: bfloat16 [16384, 1024], P(('dp', 'ep'))
- expert_ids: int32 [16384, 2], P(('dp', 'ep'))
- norm_gain: float32 [1024], replicated
- w_router: float32 [1024, 32], replicated
- w_gate: bfloat16 [32, 1024, 2816], P('ep')
- w_up: bfloat16 [32, 1024, 2816], P('ep')
- w_down: bfloat16 [32, 2816, 1024], P('ep')
Outputs:
- output 1: bfloat16 [16384, 1024], P(('dp', 'ep'))
- output 2: float32 [], replicated
- output 3: bfloat16 [16384, 1024], P(('dp', 'ep'))
- output 4: float32 [1024], replicated
- output 5: float32 [1024, 32], replicated
- output 6: bfloat16 [32, 1024, 2816], P('ep')
- output 7: bfloat16 [32, 1024, 2816], P('ep')
- output 8: bfloat16 [32, 2816, 1024], P('ep')
All inputs are finite; a program needn't handle non-finite values.
Results may differ from a plain program's by a relative error of at most 0.0152594.
Values are sent between devices in bfloat16 or wider.
A program may use at most 1.25 GiB of HBM per device.

v0:
```python
import jax
import jax.numpy as jnp
from jax import lax
from jax.sharding import PartitionSpec as P

EPS = 1e-6
AUX_COEF = 0.001


def route_tables(expert_ids, n_exp, capacity):
    flat_ids = expert_ids.reshape(-1)
    n_choice = flat_ids.shape[0]
    one_hot = (flat_ids[:, None] == jnp.arange(n_exp, dtype=jnp.int32)[None, :]).astype(jnp.int32)
    running = jnp.cumsum(one_hot, axis=0) - 1
    dest_rows = flat_ids * capacity + jnp.sum(running * one_hot, axis=1)
    slot_owner = jnp.full((n_exp * capacity,), n_choice, jnp.int32).at[dest_rows].set(jnp.arange(n_choice, dtype=jnp.int32))
    return dest_rows, slot_owner, jnp.sum(one_hot, axis=0)


def solution(mesh):
    n_dev = mesh.shape["dp"] * mesh.shape["ep"]
    all_axes = ("dp", "ep")

    def local_step(hidden, grad_out, expert_ids, norm_gain, w_router, w_gate, w_up, w_down):
        n_tok, width = hidden.shape
        n_exp = w_router.shape[1]
        capacity = 4 * n_tok // n_exp
        total_tok = n_tok * n_dev
        dest_rows, slot_owner, loads = route_tables(expert_ids, n_exp, capacity)
        choice_hot = (expert_ids[:, :, None] == jnp.arange(n_exp, dtype=jnp.int32)).astype(jnp.float32)

        x_f32 = hidden.astype(jnp.float32)
        inv_rms = lax.rsqrt(jnp.mean(x_f32 * x_f32, axis=-1, keepdims=True) + EPS)
        x_hat = x_f32 * inv_rms
        x_norm = (x_hat * norm_gain).astype(jnp.bfloat16)
        xn_f32 = x_norm.astype(jnp.float32)
        router_probs = jax.nn.softmax(jnp.dot(xn_f32, w_router, preferred_element_type=jnp.float32), axis=-1)
        gate_vals = jnp.sum(router_probs[:, None, :] * choice_hot, axis=-1)
        route_stats = lax.psum(jnp.concatenate([loads.astype(jnp.float32), jnp.sum(router_probs, axis=0)]), all_axes)
        load_frac = route_stats[:n_exp] / (2 * total_tok)
        aux_loss = AUX_COEF * n_exp * jnp.sum(load_frac * route_stats[n_exp:] / total_tok)

        send_rows = jnp.take(x_norm, slot_owner // 2, axis=0, mode="fill", fill_value=0).reshape(n_exp, capacity, width)
        recv_rows = lax.all_to_all(send_rows, "ep", 0, 1, tiled=True)
        h_gate = jnp.einsum("nrd,ndf->nrf", recv_rows, w_gate, preferred_element_type=jnp.float32).astype(jnp.bfloat16)
        h_up = jnp.einsum("nrd,ndf->nrf", recv_rows, w_up, preferred_element_type=jnp.float32).astype(jnp.bfloat16)
        gate_f32 = h_gate.astype(jnp.float32)
        up_f32 = h_up.astype(jnp.float32)
        sig_gate = jax.nn.sigmoid(gate_f32)
        silu_gate = gate_f32 * sig_gate
        act_rows = (silu_gate * up_f32).astype(jnp.bfloat16)
        exp_out = jnp.einsum("nrf,nfd->nrd", act_rows, w_down, preferred_element_type=jnp.float32).astype(jnp.bfloat16)
        back_rows = lax.all_to_all(exp_out, "ep", 1, 0, tiled=True).reshape(n_exp * capacity, width)
        picked = jnp.take(back_rows, dest_rows, axis=0).reshape(n_tok, 2, width)
        out_hidden = (x_f32 + jnp.sum(gate_vals[:, :, None] * picked, axis=1)).astype(jnp.bfloat16)

        dy_f32 = grad_out.astype(jnp.float32)
        d_gates = jnp.sum(dy_f32[:, None, :] * picked, axis=-1)
        d_picked = (dy_f32[:, None, :] * gate_vals[:, :, None]).astype(jnp.bfloat16).reshape(n_tok * 2, width)
        d_send = jnp.take(d_picked, slot_owner, axis=0, mode="fill", fill_value=0).reshape(n_exp, capacity, width)
        d_recv = lax.all_to_all(d_send, "ep", 0, 1, tiled=True)
        d_act = jnp.einsum("nrd,nfd->nrf", d_recv, w_down, preferred_element_type=jnp.float32)
        d_act = d_act.astype(jnp.bfloat16).astype(jnp.float32)
        g_down = jnp.einsum("nrf,nrd->nfd", act_rows, d_recv, preferred_element_type=jnp.float32)
        d_hup = (d_act * silu_gate).astype(jnp.bfloat16)
        d_hgate = (d_act * up_f32 * sig_gate * (1.0 + gate_f32 * (1.0 - sig_gate))).astype(jnp.bfloat16)
        g_gate = jnp.einsum("nrd,nrf->ndf", recv_rows, d_hgate, preferred_element_type=jnp.float32)
        g_up = jnp.einsum("nrd,nrf->ndf", recv_rows, d_hup, preferred_element_type=jnp.float32)
        d_rows = (jnp.einsum("nrf,ndf->nrd", d_hgate, w_gate, preferred_element_type=jnp.float32) + jnp.einsum("nrf,ndf->nrd", d_hup, w_up, preferred_element_type=jnp.float32)).astype(jnp.bfloat16)
        d_back = lax.all_to_all(d_rows, "ep", 1, 0, tiled=True).reshape(n_exp * capacity, width)
        d_xn_exp = jnp.take(d_back, dest_rows, axis=0).reshape(n_tok, 2, width)

        d_probs = jnp.sum(d_gates[:, :, None] * choice_hot, axis=1) + (AUX_COEF * n_exp / total_tok) * load_frac
        d_logits = router_probs * (d_probs - jnp.sum(router_probs * d_probs, axis=-1, keepdims=True))
        d_xnorm = jnp.einsum("te,de->td", d_logits, w_router) + d_xn_exp[:, 0].astype(jnp.float32) + d_xn_exp[:, 1].astype(jnp.float32)
        d_xnorm = d_xnorm.astype(jnp.bfloat16).astype(jnp.float32)
        value_a6 = d_xnorm * norm_gain
        grad_hidden = (inv_rms * (value_a6 - x_hat * jnp.mean(value_a6 * x_hat, axis=-1, keepdims=True)) + dy_f32).astype(jnp.bfloat16)
        small_grads = lax.psum((jnp.sum(d_xnorm * x_hat, axis=0), jnp.einsum("td,te->de", xn_f32, d_logits)), all_axes)
        big_grads = lax.psum((g_gate, g_up, g_down), "dp")
        return (out_hidden, aux_loss, grad_hidden, small_grads[0], small_grads[1], big_grads[0].astype(jnp.bfloat16), big_grads[1].astype(jnp.bfloat16), big_grads[2].astype(jnp.bfloat16))

    tok_spec = P(all_axes, None)
    w_spec = P("ep", None, None)
    return jax.shard_map(local_step, mesh=mesh, in_specs=(tok_spec, tok_spec, tok_spec, P(), P(), w_spec, w_spec, w_spec), out_specs=(tok_spec, P(), tok_spec, P(), P(), w_spec, w_spec, w_spec), check_vma=False)
```

profile of v0, /device:TPU:0, one launch (start us, length us, event | category | flops | bytes accessed | tf_op | source)
XLA Modules:
  0.0 7842.2 jit_solution(6635152915247119334)
XLA Ops:
  47.1 43.2 gather_fusion
  98.7 187.6 %all_to_all.66 = bf16[32,256,1024]{2,1,0:T(8,128)(2,1)S(1)} all-to-all(bf16[32,256,1024]{2,1,0:T(8,128)(2,1)S(1)} %broadcast_select_fusion.1), channel_id=1, replica_groups=mesh['dp'=2,'ep'=4] {'ep'}, dimensions={0} | all-to-all | bytes 33554432 | tf_op jit(solution)/shard_map/all_to_all | solution.py:44
  293.2 59.2 convolution_convert_fusion.2
  352.4 85.2 %fusion = (bf16[8,1024,2816]{2,1,0:T(8,128)(2,1)}, bf16[8,1024,2816]{2,1,0:T(8,128)(2,1)}) fusion(bf16[8,1024,2816]{2,1,0:T(8,128)(2,1)} %convolution_convert_fusion.2, bf16[8,1024,1024]{2,1,0:T(8,128)(2,1)} %bitcast.72, bf16[8,1024,2816]{2,1,0:T(8,128)(2,1)} %param.16), kind=kOutput, calls=%fused_computation.11 | convolution fusion | flops 47452258304 | bytes 201326592 | tf_op jit(solution)/shard_map/nrd,ndf->nrf/dot_general | solution.py:46
  437.5 57.9 convolution_convert_fusion.3
  495.4 18.7 copy.58
  528.9 20.6 mul.174
  553.3 150.8 %all-to-all-done.1 = bf16[8,1024,1024]{2,0,1:T(8,128)(2,1)} async-done(((bf16[8,1024,1024]{2,0,1:T(8,128)(2,1)}), bf16[8,1024,1024]{2,0,1:T(8,128)(2,1)}, u32[]{:S(2)}, u32[]{:S(2)}) %all-to-all-start.1) | async-done | bytes 16777248 | tf_op jit(solution)/shard_map/all_to_all | solution.py:53
  722.8 28.8 gather_fusion.2
  772.2 45.1 gather_fusion.1
  838.9 200.6 %psum.42 = f32[64]{0:T(128)S(1)} all-reduce(f32[64]{0:T(128)S(1)} %pad_maximum_fusion), channel_id=1, replica_groups=mesh['dp'=2,'ep'=4] {'dp','ep'}, use_global_device_ids=true, to_apply=%region_11.13 | all-reduce | flops 64 | bytes 512 | tf_op jit(solution)/shard_map/psum | solution.py:39
  1059.2 97.2 %fusion.4 = (bf16[8,1024,2816]{2,1,0:T(8,128)(2,1)}, bf16[8,1024,2816]{2,1,0:T(8,128)(2,1)}) fusion(bf16[8,1024,2816]{2,1,0:T(8,128)(2,1)} %convolution_convert_fusion.2, bf16[8,1024,2816]{2,1,0:T(8,128)(2,1)} %get-tuple-element.34, bf16[8,1024,1024]{2,1,0:T(8,128)(2,1)} %bitcast.75, bf16[8,2816,1024]{2,1,0:T(8,128)(2,1)} %param.17), kind=kOutput, calls=%fused_computation.15 | convolution fusion | flops 47636807680 | bytes 247463936 | tf_op jit(solution)/shard_map/nrd,nfd->nrf/dot_general | solution.py:62
  1156.5 55.5 fusion.38
  1211.9 68.7 fusion.39
  1280.6 69.3 fusion.41
  1350.0 68.5 fusion.40
  1418.5 56.4 add_convert_fusion
  1500.5 2074.9 %all-reduce.7 = bf16[8,2816,1024]{2,1,0:T(8,128)(2,1)} all-reduce(f32[8,2816,1024]{2,1,0:T(8,128)} %fusion.41), channel_id=1, replica_groups=mesh['dp'=2,'ep'=4] {'dp'}, use_global_device_ids=true, to_apply=%region_22.24 | all-reduce | flops 23068672 | bytes 138412032 | tf_op jit(solution)/shard_map/psum | solution.py:80
  3575.5 4074.2 %all-reduce.6 = (bf16[8,1024,2816]{2,1,0:T(8,128)(2,1)}, bf16[8,1024,2816]{2,1,0:T(8,128)(2,1)}) all-reduce(f32[8,1024,2816]{2,1,0:T(8,128)} %fusion.39, f32[8,1024,2816]{2,1,0:T(8,128)} %fusion.40), channel_id=1, replica_groups=mesh['dp'=2,'ep'=4] {'dp'}, use_global_device_ids=true, to_apply=%region_20.22 | all-reduce | flops 46137344 | bytes 276824064 | tf_op jit(solution)/shard_map/psum | solution.py:80
  7649.7 18.7 copy.64
  7668.4 28.8 gather_fusion.3
  7752.5 20.1 reshape.143
  7772.7 25.8 multiply_reduce_fusion.1
  7810.1 22.2 psum.43
  (115 shorter events, 247.5 us)
Async XLA Ops:
  7.2 542.3 %copy-start = (f32[1024,32]{0,1:T(8,128)S(1)}, f32[1024,32]{0,1:T(8,128)}, u32[]{:S(2)}) copy-start(f32[1024,32]{0,1:T(8,128)} %param.14) | copy-start | bytes 393220
  9.5 80.8 %copy-start.8 = (s32[4096]{0:T(1024)}, s32[4096]{0:T(1024)S(1)}, u32[]{:S(2)}) copy-start(s32[4096]{0:T(1024)S(1)} %eq.41) | copy-start | bytes 49156
  42.9 47.4 copy-start.16
  514.1 190.1 %all-to-all-start.1 = ((bf16[8,1024,1024]{2,0,1:T(8,128)(2,1)}), bf16[8,1024,1024]{2,0,1:T(8,128)(2,1)}, u32[]{:S(2)}, u32[]{:S(2)}) async-start(bf16[8,1024,1024]{2,0,1:T(8,128)(2,1)} %copy.58), calls=%async_computation.1 | async-start | bytes 33554432 | tf_op jit(solution)/shard_map/all_to_all | solution.py:53
  528.9 20.6 copy-start.22
  528.9 24.2 copy-start.9
  528.9 24.2 copy-start.11
  553.1 198.5 %copy-start.18 = (pred[4096]{0:T(1024)(128)(4,1)}, pred[4096]{0:T(1024)(128)(4,1)S(1)}, u32[]{:S(2)}) copy-start(pred[4096]{0:T(1024)(128)(4,1)S(1)} %compare_and_fusion.2) | copy-start | bytes 12292
  553.2 169.7 %copy-start.12 = (s32[4096]{0:T(1024)}, s32[4096]{0:T(1024)S(1)}, u32[]{:S(2)}) copy-start(s32[4096]{0:T(1024)S(1)} %broadcast_clamp_fusion.1) | copy-start | bytes 49156
  553.3 487.6 %copy-start.4 = (f32[2048,32]{0,1:T(8,128)}, f32[2048,32]{0,1:T(8,128)S(1)}, u32[]{:S(2)}) copy-start(f32[2048,32]{0,1:T(8,128)S(1)} %get-tuple-element.18) | copy-start | bytes 786436
  762.4 278.6 %copy-start.6 = (f32[2048,32]{0,1:T(8,128)}, f32[2048,32]{0,1:T(8,128)S(1)}, u32[]{:S(2)}) copy-start(f32[2048,32]{0,1:T(8,128)S(1)} %get-tuple-element.11) | copy-start | bytes 786436
  762.7 54.6 copy-start.2
  831.5 213.8 %all-to-all-start.2 = ((bf16[32,256,1024]{2,1,0:T(8,128)(2,1)}), bf16[32,256,1024]{2,1,0:T(8,128)(2,1)}, u32[]{:S(2)}, u32[]{:S(2)}) async-start(bf16[32,256,1024]{2,1,0:T(8,128)(2,1)} %broadcast_select_fusion), calls=%async_computation.2 | async-start | bytes 33554432 | tf_op jit(solution)/shard_map/all_to_all | solution.py:61
  838.5 6993.7 %all-reduce.5.cloned.1.call-start = ((), (), s32[]{:S(2)}) async-start(), calls=%async_computation.4 | async-start | bytes 262144 | tf_op jit(solution)/shard_map/psum | solution.py:79
  1040.2 19.1 copy-start.24
  1493.5 6156.2 %all-to-all-start.3 = ((bf16[8,1024,1024]{2,0,1:T(8,128)(2,1)}), bf16[8,1024,1024]{2,0,1:T(8,128)(2,1)}, u32[]{:S(2)}, u32[]{:S(2)}) async-start(bf16[8,1024,1024]{2,0,1:T(8,128)(2,1)} %copy.63), calls=%async_computation.3 | async-start | bytes 33554432 | tf_op jit(solution)/shard_map/all_to_all | solution.py:70
  7649.7 18.7 copy-start.13
  7668.4 28.8 copy-start.19
  7725.5 17.6 copy-start.7
  7725.5 17.6 copy-start.17
  7725.5 17.6 copy-start.21
  7725.5 17.6 copy-start.23
  7725.5 17.6 copy-start.25
  7752.5 20.1 copy-start.3
  (7 other events, 65.7 us)
Sparse Core Ops, SparseCore 0:
  1045.4 42.9 all-reduce.4
where the time goes:
time: 7850 us; the launch traced here: 7840 us
  blocking collectives  6560 us (84%)
  matrix products  634 us (8%)
  local copies, waits for them, and re-layouts  345 us (4%)
  waiting for transfers between devices  151 us (2%)
  other arithmetic  114 us (1%)
    psum x2, blocking collectives, local_step(): big_grads = lax.psum((g_gate, g_up, g_down), 'dp')  6150 us
    psum x1, blocking collectives, local_step(): lax.psum(jnp.concatenate([loads.astype(jnp.float32), jnp.sum(router_probs...  201 us
    all_to_all x1, blocking collectives, local_step(): recv_rows = lax.all_to_all(send_rows, 'ep', 0, 1, tiled=True)  188 us
  transfers between devices with their start and end apart: 4, of which 1 were waited for; matrix products, arithmetic and copies ran while one was open for 8% of the time, Pallas kernels for 0%

commit v1 on v0

v1 whole, which is shorter than its diff:
```python
import functools

import jax
import jax.numpy as jnp
from jax import lax
from jax.experimental import pallas as pl
from jax.experimental.pallas import tpu as pltpu
from jax.sharding import PartitionSpec as P


EPS = 1e-6
AUX_COEF = 0.001
TM = 256
CF = 256
SUB = 16
GROUP_SIZES = (3, 2, 2, 1)


def gather_kernel(scaled, src_ref, rows_ref, table_ref, tok_ref, gate_ref, out_ref):
    @pl.when(pl.program_id(1) * TM < rows_ref[pl.program_id(0)])
    def _():
        n_tok = table_ref.shape[0]
        tok = tok_ref[...]
        lane = lax.broadcasted_iota(jnp.int32, tok.shape, 1).astype(jnp.float32)
        hot = jnp.concatenate([jnp.where(tok == lane + float(j), 1.0, 0.0).astype(jnp.bfloat16) for j in range(0, n_tok, 128)], axis=1)
        got = jnp.dot(hot, table_ref[...], preferred_element_type=jnp.float32)
        if scaled:
            got = got * gate_ref[:, 0:1]
        out_ref[...] = got.astype(jnp.bfloat16)


def gather_rows(scaled, src_ids, n_rows, table, tok, gate, n_tok):
    n_src, cap = tok.shape[0], tok.shape[1]
    width = table.shape[1]
    col = pl.BlockSpec((None, TM, 128), lambda k, r, *_: (k, r, 0))
    return pl.pallas_call(
        functools.partial(gather_kernel, scaled),
        out_shape=jax.ShapeDtypeStruct((n_src, cap, width), jnp.bfloat16),
        grid_spec=pltpu.PrefetchScalarGridSpec(
            num_scalar_prefetch=2,
            grid=(n_src, cap // TM),
            in_specs=[pl.BlockSpec((n_tok, width), lambda k, r, src, *_: (src[k], 0)), col, col],
            out_specs=pl.BlockSpec((None, TM, width), lambda k, r, *_: (k, r, 0)),
        ),
        compiler_params=pltpu.CompilerParams(dimension_semantics=("arbitrary", "arbitrary"), vmem_limit_bytes=40000000),
        cost_estimate=pl.CostEstimate(flops=n_src * cap * n_tok * width, bytes_accessed=n_src * (cap + n_tok) * width * 2, transcendentals=0),
        name="gather_rows",
    )(src_ids, n_rows, table, tok, gate)


def expert_kernel(e0, n_src, n_own, n_chunk, cnt_ref, soff_ref, off_ref, xa_hbm, xb_hbm, dy_hbm, wg_ref, wu_ref, wd_ref, _gg, _gu, _gd, gg_ref, gu_ref, gd_ref, *refs):
    out_hbm, refs = refs[:n_own], refs[n_own:]
    xbuf, dobuf, xt, o_acc, dx_acc, gxs, gds, ost, dxst, load_sem, out_sem = refs
    le = pl.program_id(0)
    c = pl.program_id(1)
    n_e = pl.num_programs(0)
    e = e0 + le
    slot = lax.rem(le, 2)
    half = xa_hbm.shape[2]
    bf16 = jnp.bfloat16
    f32 = jnp.float32

    def loads(expert, slot_i, start):
        for s in range(n_src):
            n = pl.multiple_of(cnt_ref[expert, s], SUB)

            @pl.when(n > 0)
            def _():
                src = pl.ds(pl.multiple_of(soff_ref[expert, s], SUB), n)
                dst = pl.ds(pl.multiple_of(off_ref[expert, s], SUB), n)
                copies = (
                    pltpu.make_async_copy(xa_hbm.at[s, src], xbuf.at[slot_i, dst, pl.ds(0, half)], load_sem.at[0]),
                    pltpu.make_async_copy(xb_hbm.at[s, src], xbuf.at[slot_i, dst, pl.ds(half, half)], load_sem.at[2]),
                    pltpu.make_async_copy(dy_hbm.at[s, src], dobuf.at[slot_i, dst], load_sem.at[1]),
                )
                for cp in copies:
                    if start:
                        cp.start()
                    else:
                        cp.wait()

    own_rows = off_ref[e, n_own]
    tot_rows = off_ref[e, n_src]
    nt_own = lax.div(own_rows + (TM - 1), TM)
    nt = jnp.maximum(lax.div(tot_rows + (TM - 1), TM), nt_own)

    @pl.when((le == 0) & (c == 0))
    def _():
        loads(e, slot, True)

    @pl.when(c == 0)
    def _():
        loads(e, slot, False)

        @pl.when(nt > 0)
        def _():
            rows = pl.ds(pl.multiple_of((nt - 1) * TM, TM), TM)
            valid = ((nt - 1) * TM + lax.broadcasted_iota(jnp.int32, (TM, 1), 0)) < tot_rows
            for buf in (xbuf, dobuf):
                buf[slot, rows, :] = jnp.where(valid, buf[slot, rows, :].astype(f32), 0.0).astype(bf16)

        def prep(r, _):
            xt[r] = xbuf[slot, pl.ds(pl.multiple_of(r * TM, TM), TM), :].T
            return 0

        lax.fori_loop(0, nt, prep, 0)

    @pl.when((c == 1) & (le + 1 < n_e))
    def _():
        loads(e + 1, 1 - slot, True)

    @pl.when(nt == 0)
    def _():
        gxs[...] = jnp.zeros_like(gxs)
        gds[...] = jnp.zeros_like(gds)

    nt_dims = (((1,), (1,)), ((), ()))
    tn_dims = (((0,), (0,)), ((), ()))

    def tile(r, n_tile, own):
        rows = pl.ds(pl.multiple_of(r * TM, TM), n_tile * TM)
        x = xbuf[slot, rows, :]
        d_o = dobuf[slot, rows, :]
        hg = jnp.dot(x, wg_ref[...], preferred_element_type=f32).astype(bf16).astype(f32)
        hu = jnp.dot(x, wu_ref[...], preferred_element_type=f32).astype(bf16).astype(f32)
        da = lax.dot_general(d_o, wd_ref[...], nt_dims, preferred_element_type=f32).astype(bf16).astype(f32)
        sig = jax.nn.sigmoid(hg)
        silu = hg * sig
        act = (silu * hu).astype(bf16)
        dhu = (da * silu).astype(bf16)
        dhg = (da * hu * sig * (1.0 + hg * (1.0 - sig))).astype(bf16)
        both = jnp.concatenate([dhg, dhu], axis=1)
        if own:
            new = c == 0
            o_acc[rows, :] = jnp.where(new, 0.0, o_acc[rows, :]) + jnp.dot(act, wd_ref[...], preferred_element_type=f32)
            w_both = jnp.concatenate([wg_ref[...], wu_ref[...]], axis=1)
            dx_acc[rows, :] = jnp.where(new, 0.0, dx_acc[rows, :]) + lax.dot_general(both, w_both, nt_dims, preferred_element_type=f32)
        xtr = xt[r] if n_tile == 1 else jnp.concatenate([xt[r + i] for i in range(n_tile)], axis=1)
        gxs[...] = jnp.where(r == 0, 0.0, gxs[...]) + jnp.dot(xtr, both, preferred_element_type=f32)
        gds[...] = jnp.where(r == 0, 0.0, gds[...]) + lax.dot_general(act, d_o, tn_dims, preferred_element_type=f32)

    def run(lo, n, own):
        pairs = lax.div(n, 2)

        def pair(i, _):
            tile(lo + 2 * i, 2, own)
            return 0

        def single(i, _):
            tile(lo + 2 * pairs + i, 1, own)
            return 0

        lax.fori_loop(0, pairs, pair, 0)
        lax.fori_loop(0, n - 2 * pairs, single, 0)

    run(0, nt_own, True)
    run(nt_own, nt - nt_own, False)
    gg_ref[...] = gxs[:, :CF].astype(bf16)
    gu_ref[...] = gxs[:, CF:].astype(bf16)
    gd_ref[...] = gds[...].astype(bf16)

    @pl.when(c == n_chunk - 1)
    def _():
        def cast(r, _):
            rows = pl.ds(pl.multiple_of(r * TM, TM), TM)
            ost[rows, :] = o_acc[rows, :].astype(bf16)
            dxst[rows, :] = dx_acc[rows, :].astype(bf16)
            return 0

        lax.fori_loop(0, nt_own, cast, 0)
        for start in (True, False):
            for s in range(n_own):
                n = pl.multiple_of(cnt_ref[e, s], SUB)

                @pl.when(n > 0)
                def _():
                    src = pl.ds(pl.multiple_of(off_ref[e, s], SUB), n)
                    copies = (
                        pltpu.make_async_copy(ost.at[src], out_hbm[s].at[0, le, pl.ds(0, n)], out_sem.at[0]),
                        pltpu.make_async_copy(dxst.at[src], out_hbm[s].at[1, le, pl.ds(0, n)], out_sem.at[1]),
                    )
                    for cp in copies:
                        if start:
                            cp.start()
                        else:
                            cp.wait()


def run_experts(e0, n_e, cnt, soff, off, x_src, dy_src, seg_cap, w_gate, w_up, w_down, prev):
    n_src, cap, width = dy_src.shape
    n_loc = w_gate.shape[0]
    n_own = n_src // 2
    ff = w_gate.shape[2]
    n_chunk = ff // CF
    own_cap = n_own * seg_cap
    bf16 = jnp.bfloat16
    f32 = jnp.float32
    col_spec = pl.BlockSpec((None, width, CF), lambda i, c, *_: (e0 + i, 0, c))
    row_spec = pl.BlockSpec((None, CF, width), lambda i, c, *_: (e0 + i, c, 0))
    any_spec = pl.BlockSpec(memory_space=pl.ANY)
    first = prev is None
    if first:
        prev = (jnp.zeros((8, 128), bf16),) * 3
    out_shape = (
        jax.ShapeDtypeStruct((n_loc, width, ff), bf16),
        jax.ShapeDtypeStruct((n_loc, width, ff), bf16),
        jax.ShapeDtypeStruct((n_loc, ff, width), bf16),
    ) + (jax.ShapeDtypeStruct((2, n_e, seg_cap, width), bf16),) * n_own
    rows_est = n_e * cap // 2
    n_in = 9
    return pl.pallas_call(
        functools.partial(expert_kernel, e0, n_src, n_own, n_chunk),
        out_shape=out_shape,
        grid_spec=pltpu.PrefetchScalarGridSpec(
            num_scalar_prefetch=3,
            grid=(n_e, n_chunk),
            in_specs=[any_spec] * 3 + [col_spec, col_spec, row_spec] + [any_spec] * 3,
            out_specs=[col_spec, col_spec, row_spec] + [any_spec] * n_own,
            scratch_shapes=[
                pltpu.VMEM((2, cap, width), bf16),
                pltpu.VMEM((2, cap, width), bf16),
                pltpu.VMEM((cap // TM, width, TM), bf16),
                pltpu.VMEM((own_cap, width), f32),
                pltpu.VMEM((own_cap, width), f32),
                pltpu.VMEM((width, 2 * CF), f32),
                pltpu.VMEM((CF, width), f32),
                pltpu.VMEM((own_cap, width), bf16),
                pltpu.VMEM((own_cap, width), bf16),
                pltpu.SemaphoreType.DMA((3,)),
                pltpu.SemaphoreType.DMA((2,)),
            ],
        ),
        input_output_aliases={} if first else {n_in: 0, n_in + 1: 1, n_in + 2: 2},
        compiler_params=pltpu.CompilerParams(dimension_semantics=("arbitrary", "arbitrary"), vmem_limit_bytes=64000000),
        cost_estimate=pl.CostEstimate(flops=2 * 9 * rows_est * width * ff, bytes_accessed=n_e * width * ff * 12, transcendentals=0),
        name="experts",
    )(cnt, soff, off, *x_src, dy_src, w_gate, w_up, w_down, *prev)


def solution(mesh):
    n_dp, n_ep = mesh.shape["dp"], mesh.shape["ep"]
    n_dev = n_dp * n_ep
    all_axes = ("dp", "ep")

    def local_body(hidden, grad_out, expert_ids, norm_gain, w_router, w_gate, w_up, w_down):
        n_tok, width = hidden.shape
        n_exp = w_router.shape[1]
        n_loc = n_exp // n_ep
        capacity = 4 * n_tok // n_exp
        total_tok = n_tok * n_dev
        f32 = jnp.float32
        d_ix, e_ix = lax.axis_index("dp"), lax.axis_index("ep")

        dy_all = lax.all_gather(grad_out, all_axes, axis=0, tiled=True)

        x_f32 = hidden.astype(f32)
        inv_rms = lax.rsqrt(jnp.mean(x_f32 * x_f32, axis=-1, keepdims=True) + EPS)
        x_hat = x_f32 * inv_rms
        x_norm = (x_hat * norm_gain).astype(jnp.bfloat16)
        half = width // 2
        xa_all = lax.all_gather(x_norm[:, :half], all_axes, axis=0, tiled=True)
        xb_all = lax.all_gather(x_norm[:, half:], all_axes, axis=0, tiled=True)
        xn_f32 = x_norm.astype(f32)
        choice_hot = (expert_ids[:, :, None] == jnp.arange(n_exp, dtype=jnp.int32)).astype(f32)
        router_probs = jax.nn.softmax(jnp.dot(xn_f32, w_router, preferred_element_type=f32), axis=-1)
        gate_vals = jnp.sum(router_probs[:, None, :] * choice_hot, axis=-1)

        flat_ids = expert_ids.reshape(-1)
        one_hot = (flat_ids[:, None] == jnp.arange(n_exp, dtype=jnp.int32)[None, :]).astype(jnp.int32)
        running = jnp.cumsum(one_hot, axis=0) - 1
        dest_rows = flat_ids * capacity + jnp.sum(running * one_hot, axis=1)
        counts = jnp.sum(one_hot, axis=0)
        tokens = lax.broadcasted_iota(f32, (n_tok, 2), 0).reshape(-1)
        pair = jnp.stack([tokens, gate_vals.reshape(-1)], axis=1)
        n_slot = n_exp * capacity
        owner_rows = n_loc * capacity
        padded = (counts + (SUB - 1)) // SUB * SUB
        per_owner = padded.reshape(n_ep, n_loc)
        seg_off = (jnp.cumsum(per_owner, axis=1) - per_owner + owner_rows * jnp.arange(n_ep, dtype=jnp.int32)[:, None]).reshape(-1)
        packed = jnp.sum((running + seg_off[None, :]) * one_hot, axis=1)
        slots = jnp.broadcast_to(jnp.array([-1.0, 0.0], f32), (n_slot, 2)).at[packed].set(pair, unique_indices=True)
        slot_tok = slots[:, 0]
        slot_gate = slots[:, 1]
        mine = jnp.concatenate([slot_tok, slot_gate, counts.astype(f32), jnp.sum(router_probs, axis=0), jnp.zeros((64,), f32)])
        table = lax.all_gather(mine, all_axes, axis=0, tiled=False)
        route_stats = jnp.sum(table[:, 2 * n_slot:2 * n_slot + 2 * n_exp], axis=0)
        load_frac = route_stats[:n_exp] / (2 * total_tok)
        aux_loss = AUX_COEF * n_exp * jnp.sum(load_frac * route_stats[n_exp:] / total_tok)

        src_ids = [lax.rem(d_ix + k // n_ep, n_dp) * n_ep + lax.rem(e_ix + k % n_ep, n_ep) for k in range(n_dev)]
        mine_of = [lax.dynamic_index_in_dim(table, s, 0, keepdims=False) for s in src_ids]

        def cols(lo):
            part = jnp.stack([lax.dynamic_slice_in_dim(t, lo + e_ix * owner_rows, owner_rows, axis=0) for t in mine_of])
            return jnp.broadcast_to(part[..., None], (n_dev, owner_rows, 128))

        tok_col, gate_col = cols(0), cols(n_slot)
        cnt = jnp.stack([lax.dynamic_slice_in_dim(t, 2 * n_slot + e_ix * n_loc, n_loc, axis=0) for t in mine_of], axis=1).astype(jnp.int32)
        cnt = (cnt + (SUB - 1)) // SUB * SUB
        soff = jnp.cumsum(cnt, axis=0) - cnt
        off = jnp.concatenate([jnp.zeros((n_loc, 1), jnp.int32), jnp.cumsum(cnt, axis=1)], axis=1)
        n_rows = jnp.sum(cnt, axis=0)
        src_vec = jnp.stack(src_ids).astype(jnp.int32)
        dy_src = gather_rows(True, src_vec, n_rows, dy_all, tok_col, gate_col, n_tok)
        xa_all, dy_src = lax.optimization_barrier((xa_all, dy_src))
        xa_src = gather_rows(False, src_vec, n_rows, xa_all, tok_col, gate_col, n_tok)
        xb_all, xa_src = lax.optimization_barrier((xb_all, xa_src))
        x_src = (xa_src, gather_rows(False, src_vec, n_rows, xb_all, tok_col, gate_col, n_tok))

        prev = None
        backs = [[] for _ in range(n_ep)]
        e0 = 0
        for per in GROUP_SIZES:
            outs = run_experts(e0, per, cnt, soff, off, x_src, dy_src, capacity, w_gate, w_up, w_down, prev)
            prev = outs[:3]
            e0 += per
            for k in range(n_ep):
                sent = outs[3 + k]
                moved = sent
                if k > 0:
                    ring = [(i, (i + k) % n_ep) for i in range(n_ep)]
                    if e0 < n_loc:
                        moved = lax.ppermute(sent, "ep", ring)
                    else:
                        moved = (lax.ppermute(sent[0], "ep", ring), lax.ppermute(sent[1], "ep", ring))
                backs[k].append(moved)
        g_gate, g_up, g_down = prev
        back_rows = jnp.concatenate([b[0] for bk in backs for b in bk], axis=0).reshape(n_slot, width)
        d_back = jnp.concatenate([b[1] for bk in backs for b in bk], axis=0).reshape(n_slot, width)
        owner = dest_rows // owner_rows
        back_ix = (lax.rem(e_ix - owner + n_ep, n_ep) * owner_rows + lax.rem(dest_rows, owner_rows)).reshape(n_tok, 2)

        def picks(rows):
            return [rows.at[back_ix[:, j]].get(mode="promise_in_bounds").astype(f32) for j in range(2)]

        picked = picks(back_rows)
        out_hidden = (x_f32 + (gate_vals[:, 0:1] * picked[0] + gate_vals[:, 1:2] * picked[1])).astype(jnp.bfloat16)
        dy_f32 = grad_out.astype(f32)
        d_gates = jnp.stack([jnp.sum(dy_f32 * p, axis=-1) for p in picked], axis=1)
        d_xn_exp = picks(d_back)

        d_probs = jnp.sum(d_gates[:, :, None] * choice_hot, axis=1) + (AUX_COEF * n_exp / total_tok) * load_frac
        d_logits = router_probs * (d_probs - jnp.sum(router_probs * d_probs, axis=-1, keepdims=True))
        d_xnorm = jnp.einsum("te,de->td", d_logits, w_router) + d_xn_exp[0] + d_xn_exp[1]
        d_xnorm = d_xnorm.astype(jnp.bfloat16).astype(f32)
        scaled = d_xnorm * norm_gain
        grad_hidden = (inv_rms * (scaled - x_hat * jnp.mean(scaled * x_hat, axis=-1, keepdims=True)) + dy_f32).astype(jnp.bfloat16)
        grad_router = lax.psum(jnp.einsum("td,te->de", xn_f32, d_logits), all_axes)
        grad_gain = lax.psum(jnp.sum(d_xnorm * x_hat, axis=0), all_axes)
        return (out_hidden, aux_loss, grad_hidden, grad_gain, grad_router, g_gate, g_up, g_down)

    tok_spec = P(all_axes, None)
    w_spec = P("ep", None, None)
    return jax.shard_map(local_body, mesh=mesh, in_specs=(tok_spec, tok_spec, tok_spec, P(), P(), w_spec, w_spec, w_spec), out_specs=(tok_spec, P(), tok_spec, P(), P(), w_spec, w_spec, w_spec), check_vma=False)
```

time: 7850 us -> 1500 us (0.19)
  blocking collectives: 6560 us -> 43.5 us
  Pallas kernels: 0 us -> 894 us
  matrix products: 634 us -> 10.2 us
  local copies, waits for them, and re-layouts: 345 us -> 172 us
  waiting for transfers between devices: 151 us -> 298 us
    psum x4 -> x1, blocking collectives: 6370 us -> 24.1 us  [local_body(): grad_gain = lax.psum(jnp.sum(d_xnorm * x_hat, axis=0), all_axes)]
    pallas_call x0 -> x7, Pallas kernels: none -> 894 us  [the longest x4 694 us: run_experts(): pl.pallas_call(functools.partial(expert_kernel, e0, n_src, n_own, n_chunk...]
    dot_general x12 -> x3, matrix products: 634 us -> 10.2 us  [the longest x1 4.58 us: local_body(): jnp.einsum('te,de->td', d_logits, w_router) + d_xn_exp[0] + d_xn_exp[1]]
    ppermute x0 -> x15, waiting for transfers between devices: none -> 196 us  [the longest x9 117 us: local_body(): moved = lax.ppermute(sent, 'ep', ring)]
    all_to_all x1 -> x0, blocking collectives: 188 us -> none  [local_step(): recv_rows = lax.all_to_all(send_rows, 'ep', 0, 1, tiled=True)]
    all_to_all x3 -> x0, waiting for transfers between devices: 151 us -> none  [the longest x1 151 us: local_step(): lax.all_to_all(exp_out, 'ep', 1, 0, tiled=True)]
    all_gather x0 -> x3, waiting for transfers between devices: none -> 93.8 us  [the longest x1 78.3 us: local_body(): dy_all = lax.all_gather(grad_out, all_axes, axis=0, tiled=True)]
  transfers between devices with their start and end apart: 4 -> 19, of which waited for: 1 -> 10; matrix products, arithmetic and copies ran while one was open for 8% -> 8% of each run, Pallas kernels for 0% -> 37%
where the time goes in v1:
time: 1500 us; the launch traced here: 1490 us
  Pallas kernels  894 us (60%)
  waiting for transfers between devices  298 us (20%)
  local copies, waits for them, and re-layouts  172 us (11%)
  blocking collectives  43.5 us (3%)
  other arithmetic  43.1 us (3%)
  between operations  16.6 us (1%)
    pallas_call x4, Pallas kernels, run_experts(): pl.pallas_call(functools.partial(expert_kernel, e0, n_src, n_own, n_chunk...  694 us
    pallas_call x3, Pallas kernels, gather_rows(): pl.pallas_call(functools.partial(gather_kernel, scaled), out_shape=jax.Sh...  201 us
    ppermute x9, waiting for transfers between devices, local_body(): moved = lax.ppermute(sent, 'ep', ring)  117 us
    all_gather x1, waiting for transfers between devices, local_body(): dy_all = lax.all_gather(grad_out, all_axes, axis=0, tiled=True)  78.3 us
    gather x4, local copies, waits for them, and re-layouts, picks(): rows.at[back_ix[:, j]].get(mode='promise_in_bounds').astype(f32)  75.6 us
    unnamed x89, local copies, waits for them, and re-layouts  50.5 us
    ppermute x3, waiting for transfers between devices, local_body(): lax.ppermute(sent[0], 'ep', ring)  48.1 us
    ppermute x3, waiting for transfers between devices, local_body(): lax.ppermute(sent[1], 'ep', ring)  31.2 us
  transfers between devices with their start and end apart: 19, of which 10 were waited for; matrix products, arithmetic and copies ran while one was open for 8% of the time, Pallas kernels for 37%

profile of v1, /device:TPU:0, one launch (start us, length us, event | category | flops | bytes accessed | tf_op | source)
XLA Modules:
  0.0 1489.0 jit_solution(12668560987768993210)
XLA Ops:
  30.0 9.2 reduce-window.6
  43.3 15.2 %scatter_fusion = f32[8192,2]{1,0:T(8,128)} fusion(f32[8192,2]{1,0:T(8,128)} %broadcast_in_dim.10, s32[4096]{0:T(1024)S(1)} %bitcast.202, f32[4096,2]{1,0:T(8,128)S(1)} %copy.104), kind=kCustom, calls=%fused_computation.4 | custom fusion | bytes 114688 | tf_op jit(solution)/shard_map/scatter | solution.py:281
  65.5 19.4 %all-gather.1 = f32[8,1,16512]{2,1,0:T(1,128)S(1)} all-gather(f32[1,1,16512]{2,1,0:T(1,128)S(1)} %reshape.211), channel_id=2, replica_groups=mesh['dp'=2,'ep'=4] {'dp','ep'}, dimensions={0}, use_global_device_ids=true | all-gather | bytes 594432 | tf_op jit(solution)/shard_map/all_gather | solution.py:285
  92.4 78.3 %all-gather.10.cloned.1.call-done.table_ref = bf16[16384,1024]{1,0:T(8,128)(2,1)} async-done(((bf16[2048,1024]{1,0:T(8,128)(2,1)}), bf16[16384,1024]{1,0:T(8,128)(2,1)}) %all-gather.10.cloned.1.call-update) | async-done | bytes 33554448 | tf_op jit(solution)/shard_map/all_gather | solution.py:254
  177.5 84.3 %gather_rows.3.dy_hbm = bf16[8,2048,1024]{2,1,0:T(8,128)(2,1)} custom-call(s32[8]{0:T(128)S(1)} %stack.106.src_ref, s32[8]{0:T(128)S(1)} %get-tuple-element.81.rows_ref, bf16[16384,1024]{1,0:T(8,128)(2,1)} %all-gather.10.cloned.1.call-done.table_ref, f32[8,2048,128]{2,1,0:T(8,128)S(1)} %broadcast_in_dim.12.tok_ref, f32[8,2048,128]{2,1,0:T(8,128)} %broadcast_in_dim.13.gate_ref), custom_call_target="tpu_custom_call" | custom-call | flops 34359738368 | bytes 67108864 | tf_op jit(solution)/shard_map/gather_rows/pallas_call | solution.py:36
  270.2 58.3 %gather_rows.4.xa_hbm = bf16[8,2048,512]{2,1,0:T(8,128)(2,1)} custom-call(s32[8]{0:T(128)S(1)} %stack.106.src_ref, s32[8]{0:T(128)S(1)} %get-tuple-element.81.rows_ref, bf16[16384,512]{1,0:T(8,128)(2,1)} %all-gather.8.cloned.1.call-done.table_ref, f32[8,2048,128]{2,1,0:T(8,128)S(1)} %copy-done.2, f32[8,2048,128]{2,1,0:T(8,128)} %broadcast_in_dim.13.gate_ref), custom_call_target="tpu_custom_call" | custom-call | flops 17179869184 | bytes 33554432 | tf_op jit(solution)/shard_map/gather_rows/pallas_call | solution.py:36
  328.4 15.5 %all-gather.6.cloned.1.call-done.table_ref = bf16[16384,512]{1,0:T(8,128)(2,1)} async-done(((bf16[2048,512]{1,0:T(8,128)(2,1)}), bf16[16384,512]{1,0:T(8,128)(2,1)}) %all-gather.6.cloned.1.call-update) | async-done | bytes 16777232 | tf_op jit(solution)/shard_map/all_gather | solution.py:262
  347.3 58.2 %gather_rows.5.xb_hbm = bf16[8,2048,512]{2,1,0:T(8,128)(2,1)} custom-call(s32[8]{0:T(128)S(1)} %stack.106.src_ref, s32[8]{0:T(128)S(1)} %get-tuple-element.81.rows_ref, bf16[16384,512]{1,0:T(8,128)(2,1)} %all-gather.6.cloned.1.call-done.table_ref, f32[8,2048,128]{2,1,0:T(8,128)S(1)} %copy-done.3, f32[8,2048,128]{2,1,0:T(8,128)} %broadcast_in_dim.13.gate_ref), custom_call_target="tpu_custom_call" | custom-call | flops 17179869184 | bytes 33554432 | tf_op jit(solution)/shard_map/gather_rows/pallas_call | solution.py:36
  406.0 278.7 %experts.4 = (bf16[8,1024,2816]{2,1,0:T(8,128)(2,1)}, bf16[8,1024,2816]{2,1,0:T(8,128)(2,1)}, bf16[8,2816,1024]{2,1,0:T(8,128)(2,1)}, bf16[2,3,256,1024]{3,2,1,0...) custom-call(s32[8,8]{1,0:T(8,128)} %copy-done.19, ...), custom_call_target="tpu_custom_call" | custom-call | flops 159450660864 | bytes 103809024 | tf_op jit(solution)/shard_map/experts/pallas_call | solution.py:211
  684.8 172.2 %experts.5 = (bf16[8,1024,2816]{2,1,0:T(8,128)(2,1)}, bf16[8,1024,2816]{2,1,0:T(8,128)(2,1)}, bf16[8,2816,1024]{2,1,0:T(8,128)(2,1)}, bf16[2,2,256,1024]{3,2,1,0...) custom-call(s32[8,8]{1,0:T(8,128)} %copy-done.19, ...), custom_call_target="tpu_custom_call", output_to_operand_aliasing={{0}: (9, {}), {1}: (10, {}), {2}: (11, {})} | custom-call | flops 106300440576 | bytes 69206016 | tf_op jit(solution)/shard_map/experts/pallas_call | solution.py:211
  857.1 155.7 %experts.6 = (bf16[8,1024,2816]{2,1,0:T(8,128)(2,1)}, bf16[8,1024,2816]{2,1,0:T(8,128)(2,1)}, bf16[8,2816,1024]{2,1,0:T(8,128)(2,1)}, bf16[2,2,256,1024]{3,2,1,0...) custom-call(s32[8,8]{1,0:T(8,128)} %copy-done.19, ...), custom_call_target="tpu_custom_call", output_to_operand_aliasing={{0}: (9, {}), {1}: (10, {}), {2}: (11, {})} | custom-call | flops 106300440576 | bytes 69206016 | tf_op jit(solution)/shard_map/experts/pallas_call | solution.py:211
  1012.8 87.0 %experts.7 = (bf16[8,1024,2816]{2,1,0:T(8,128)(2,1)}, bf16[8,1024,2816]{2,1,0:T(8,128)(2,1)}, bf16[8,2816,1024]{2,1,0:T(8,128)(2,1)}, bf16[2,1,256,1024]{3,2,1,0...) custom-call(s32[8,8]{1,0:T(8,128)} %copy-done.19, ...), custom_call_target="tpu_custom_call", output_to_operand_aliasing={{0}: (9, {}), {1}: (10, {}), {2}: (11, {})} | custom-call | flops 53150220288 | bytes 34603008 | tf_op jit(solution)/shard_map/experts/pallas_call | solution.py:211
  1112.8 25.2 %collective-permute-done.12 = bf16[1,256,1024]{2,1,0:T(8,128)(2,1)S(1)} collective-permute-done((bf16[1,256,1024]{2,1,0:T(8,128)(2,1)S(1)}, bf16[1,256,1024]{2,1,0:T(8,128)(2,1)S(1)}, u32[]{:S(2)}, u32[]{:S(2)}) %collective-permute-start.12) | collective-permute-done | bytes 524320 | tf_op jit(solution)/shard_map/ppermute | solution.py:325
  1161.4 94.1 %collective-permute-done.5 = bf16[2,2,256,1024]{3,2,1,0:T(8,128)(2,1)S(1)} collective-permute-done((bf16[2,2,256,1024]{3,2,1,0:T(8,128)(2,1)S(1)}, bf16[2,2,256,1024]{3,2,1,0:T(8,128)(2,1)S(1)}, u32[]{:S(2)}, u32[]{:S(2)}) %collective-permute-start.5) | collective-permute-done | bytes 2097184 | tf_op jit(solution)/shard_map/ppermute | solution.py:323
  1255.5 22.5 %collective-permute-done.6 = bf16[2,2,256,1024]{3,2,1,0:T(8,128)(2,1)S(1)} collective-permute-done((bf16[2,2,256,1024]{3,2,1,0:T(8,128)(2,1)S(1)}, bf16[2,2,256,1024]{3,2,1,0:T(8,128)(2,1)S(1)}, u32[]{:S(2)}, u32[]{:S(2)}) %collective-permute-start.6) | collective-permute-done | bytes 2097184 | tf_op jit(solution)/shard_map/ppermute | solution.py:323
  1281.0 47.5 %collective-permute-done.7 = bf16[1,256,1024]{2,1,0:T(8,128)(2,1)S(1)} collective-permute-done((bf16[1,256,1024]{2,1,0:T(8,128)(2,1)S(1)}, bf16[1,256,1024]{2,1,0:T(8,128)(2,1)S(1)}, u32[]{:S(2)}, u32[]{:S(2)}) %collective-permute-start.7) | collective-permute-done | bytes 524320 | tf_op jit(solution)/shard_map/ppermute | solution.py:325
  1342.5 18.9 %gather_fusion.1 = bf16[2048,1024]{1,0:T(8,128)(2,1)} fusion(bf16[8192,1024]{1,0:T(8,128)(2,1)} %bitcast.52, s32[2048]{0:T(1024)S(1)} %get-tuple-element.156), kind=kCustom, calls=%fused_computation.1 | custom fusion | bytes 8396800 | tf_op jit(solution)/shard_map/gather | solution.py:334
  1361.3 18.9 %gather_fusion = bf16[2048,1024]{1,0:T(8,128)(2,1)} fusion(bf16[8192,1024]{1,0:T(8,128)(2,1)} %bitcast.52, s32[2048]{0:T(1024)S(1)} %get-tuple-element.157), kind=kCustom, calls=%fused_computation | custom fusion | bytes 8396800 | tf_op jit(solution)/shard_map/gather | solution.py:334
  1380.2 10.3 fusion.12
  1396.8 19.0 %gather_fusion.2 = bf16[2048,1024]{1,0:T(8,128)(2,1)} fusion(bf16[8192,1024]{1,0:T(8,128)(2,1)} %bitcast.74, s32[2048]{0:T(1024)S(1)} %get-tuple-element.157), kind=kCustom, calls=%fused_computation.2 | custom fusion | bytes 8396800 | tf_op jit(solution)/shard_map/gather | solution.py:334
  1415.8 18.9 %gather_fusion.3 = bf16[2048,1024]{1,0:T(8,128)(2,1)} fusion(bf16[8192,1024]{1,0:T(8,128)(2,1)} %bitcast.74, s32[2048]{0:T(1024)S(1)} %get-tuple-element.156), kind=kCustom, calls=%fused_computation.3 | custom fusion | bytes 8396800 | tf_op jit(solution)/shard_map/gather | solution.py:334
  1434.8 9.2 fusion.9
  1448.3 24.1 %psum.14 = f32[1024]{0:T(1024)} all-reduce(f32[1024]{0:T(1024)S(1)} %get-tuple-element.72), channel_id=1, replica_groups=mesh['dp'=2,'ep'=4] {'dp','ep'}, use_global_device_ids=true, to_apply=%region_23.24 | all-reduce | flops 1024 | bytes 8192 | tf_op jit(solution)/shard_map/psum | solution.py:349
  1472.4 7.2 all-reduce.3.cloned.1.call-done
  (201 shorter events, 125.0 us)
Async XLA Ops:
  7.2 163.5 %all-gather.10.cloned.1.call-start = ((), (), s32[]{:S(2)}) async-start(), calls=%async_computation.2 | async-start | bytes 37748736 | tf_op jit(solution)/shard_map/all_gather | solution.py:254
  7.9 258.1 %all-gather.8.cloned.1.call-start = ((), (), s32[]{:S(2)}) async-start(), calls=%async_computation.1 | async-start | bytes 18874368 | tf_op jit(solution)/shard_map/all_gather | solution.py:261
  19.3 324.6 %all-gather.6.cloned.1.call-start = ((), (), s32[]{:S(2)}) async-start(), calls=%async_computation | async-start | bytes 18874368 | tf_op jit(solution)/shard_map/all_gather | solution.py:262
  20.0 1459.6 %all-reduce.3.cloned.1.call-start = ((), (), s32[]{:S(2)}) async-start(), calls=%async_computation.3 | async-start | bytes 262144 | tf_op jit(solution)/shard_map/psum | solution.py:348
  85.7 91.8 %copy-start.19 = (s32[8,8]{1,0:T(8,128)}, s32[8,8]{1,0:T(8,128)S(1)}, u32[]{:S(2)}) copy-start(s32[8,8]{1,0:T(8,128)S(1)} %get-tuple-element.82.cnt_ref) | copy-start | bytes 772
  684.7 457.0 %collective-permute-start = (bf16[2,3,256,1024]{3,2,1,0:T(8,128)(2,1)}, bf16[2,3,256,1024]{3,2,1,0:T(8,128)(2,1)}, u32[]{:S(2)}, u32[]{:S(2)}) collective-permute-start(bf16[2,3,256,1024]{3,2,1,0:T(8,128)(2,1)} %get-tuple-element.57), channel_id=1, source_target_pairs={{0,1},{1,2},{2,3},{3,0},{4,5},{5,6},{6,7},{7,4}} | collective-permute-start | bytes 9437192 | tf_op jit(solution)/shard_map/ppermute | solution.py:323
  857.0 281.1 %collective-permute-start.1 = (bf16[2,2,256,1024]{3,2,1,0:T(8,128)(2,1)}, bf16[2,2,256,1024]{3,2,1,0:T(8,128)(2,1)}, u32[]{:S(2)}, u32[]{:S(2)}) collective-permute-start(bf16[2,2,256,1024]{3,2,1,0:T(8,128)(2,1)} %get-tuple-element.58), channel_id=1, source_target_pairs={{0,1},{1,2},{2,3},{3,0},{4,5},{5,6},{6,7},{7,4}} | collective-permute-start | bytes 6291464 | tf_op jit(solution)/shard_map/ppermute | solution.py:323
  857.0 297.8 %collective-permute-start.4 = (bf16[2,3,256,1024]{3,2,1,0:T(8,128)(2,1)}, bf16[2,3,256,1024]{3,2,1,0:T(8,128)(2,1)}, u32[]{:S(2)}, u32[]{:S(2)}) collective-permute-start(bf16[2,3,256,1024]{3,2,1,0:T(8,128)(2,1)} %get-tuple-element.61), channel_id=1, source_target_pairs={{0,2},{1,3},{2,0},{3,1},{4,6},{5,7},{6,4},{7,5}} | collective-permute-start | bytes 9437192 | tf_op jit(solution)/shard_map/ppermute | solution.py:323
  1012.7 88.6 %copy-start.24 = (s32[2048,1]{0,1:T(1,128)S(1)}, s32[2048,1]{0,1:T(1,128)}, u32[]{:S(2)}) copy-start(s32[2048,1]{0,1:T(1,128)} %get-tuple-element.146) | copy-start | bytes 24580
  1012.8 88.6 %copy-start.25 = (s32[2048,1]{0,1:T(1,128)S(1)}, s32[2048,1]{0,1:T(1,128)}, u32[]{:S(2)}) copy-start(s32[2048,1]{0,1:T(1,128)} %get-tuple-element.147) | copy-start | bytes 24580
  1012.8 88.6 %copy-start.33 = (bf16[2,2,256,1024]{3,2,1,0:T(8,128)(2,1)S(1)}, bf16[2,2,256,1024]{3,2,1,0:T(8,128)(2,1)}, u32[]{:S(2)}) copy-start(bf16[2,2,256,1024]{3,2,1,0:T(8,128)(2,1)} %get-tuple-element.59) | copy-start | bytes 6291460
  1099.8 42.0 %copy-start.10 = (bf16[2,2,256,1024]{3,2,1,0:T(8,128)(2,1)S(1)}, bf16[2,2,256,1024]{3,2,1,0:T(8,128)(2,1)}, u32[]{:S(2)}) copy-start(bf16[2,2,256,1024]{3,2,1,0:T(8,128)(2,1)} %get-tuple-element.52) | copy-start | bytes 6291460
  1101.3 8.6 collective-permute-start.3
  1101.3 50.4 %collective-permute-start.2 = (bf16[2,2,256,1024]{3,2,1,0:T(8,128)(2,1)S(1)}, bf16[2,2,256,1024]{3,2,1,0:T(8,128)(2,1)S(1)}, u32[]{:S(2)}, u32[]{:S(2)}) collective-permute-start(bf16[2,2,256,1024]{3,2,1,0:T(8,128)(2,1)S(1)} %copy-done.33), channel_id=1, source_target_pairs={{0,1},{1,2},{2,3},{3,0},{4,5},{5,6},{6,7},{7,4}} | collective-permute-start | bytes 6291464 | tf_op jit(solution)/shard_map/ppermute | solution.py:323
  1109.9 28.1 %collective-permute-start.12 = (bf16[1,256,1024]{2,1,0:T(8,128)(2,1)S(1)}, bf16[1,256,1024]{2,1,0:T(8,128)(2,1)S(1)}, u32[]{:S(2)}, u32[]{:S(2)}) collective-permute-start(bf16[1,256,1024]{2,1,0:T(8,128)(2,1)S(1)} %get-tuple-element.116), channel_id=1, source_target_pairs={{0,1},{1,2},{2,3},{3,0},{4,5},{5,6},{6,7},{7,4}} | collective-permute-start | bytes 1572872 | tf_op jit(solution)/shard_map/ppermute | solution.py:325
  1138.0 197.0 %collective-permute-start.8 = (bf16[2,3,256,1024]{3,2,1,0:T(8,128)(2,1)S(1)}, bf16[2,3,256,1024]{3,2,1,0:T(8,128)(2,1)S(1)}, u32[]{:S(2)}, u32[]{:S(2)}) collective-permute-start(bf16[2,3,256,1024]{3,2,1,0:T(8,128)(2,1)S(1)} %copy-done.28), channel_id=1, source_target_pairs={{0,3},{1,0},{2,1},{3,2},{4,7},{5,4},{6,5},{7,6}} | collective-permute-start | bytes 9437192 | tf_op jit(solution)/shard_map/ppermute | solution.py:323
  1138.1 117.4 %collective-permute-start.5 = (bf16[2,2,256,1024]{3,2,1,0:T(8,128)(2,1)S(1)}, bf16[2,2,256,1024]{3,2,1,0:T(8,128)(2,1)S(1)}, u32[]{:S(2)}, u32[]{:S(2)}) collective-permute-start(bf16[2,2,256,1024]{3,2,1,0:T(8,128)(2,1)S(1)} %copy-done.31), channel_id=1, source_target_pairs={{0,2},{1,3},{2,0},{3,1},{4,6},{5,7},{6,4},{7,5}} | collective-permute-start | bytes 6291464 | tf_op jit(solution)/shard_map/ppermute | solution.py:323
  1141.8 136.2 %collective-permute-start.6 = (bf16[2,2,256,1024]{3,2,1,0:T(8,128)(2,1)S(1)}, bf16[2,2,256,1024]{3,2,1,0:T(8,128)(2,1)S(1)}, u32[]{:S(2)}, u32[]{:S(2)}) collective-permute-start(bf16[2,2,256,1024]{3,2,1,0:T(8,128)(2,1)S(1)} %copy-done.32), channel_id=1, source_target_pairs={{0,2},{1,3},{2,0},{3,1},{4,6},{5,7},{6,4},{7,5}} | collective-permute-start | bytes 6291464 | tf_op jit(solution)/shard_map/ppermute | solution.py:323
  1151.8 185.3 %collective-permute-start.9 = (bf16[2,2,256,1024]{3,2,1,0:T(8,128)(2,1)S(1)}, bf16[2,2,256,1024]{3,2,1,0:T(8,128)(2,1)S(1)}, u32[]{:S(2)}, u32[]{:S(2)}) collective-permute-start(bf16[2,2,256,1024]{3,2,1,0:T(8,128)(2,1)S(1)} %copy-done.29), channel_id=1, source_target_pairs={{0,3},{1,0},{2,1},{3,2},{4,7},{5,4},{6,5},{7,6}} | collective-permute-start | bytes 6291464 | tf_op jit(solution)/shard_map/ppermute | solution.py:323
  1154.8 183.7 %collective-permute-start.10 = (bf16[2,2,256,1024]{3,2,1,0:T(8,128)(2,1)S(1)}, bf16[2,2,256,1024]{3,2,1,0:T(8,128)(2,1)S(1)}, u32[]{:S(2)}, u32[]{:S(2)}) collective-permute-start(bf16[2,2,256,1024]{3,2,1,0:T(8,128)(2,1)S(1)} %copy-done.30), channel_id=1, source_target_pairs={{0,3},{1,0},{2,1},{3,2},{4,7},{5,4},{6,5},{7,6}} | collective-permute-start | bytes 6291464 | tf_op jit(solution)/shard_map/ppermute | solution.py:323
  1255.5 73.0 %collective-permute-start.7 = (bf16[1,256,1024]{2,1,0:T(8,128)(2,1)S(1)}, bf16[1,256,1024]{2,1,0:T(8,128)(2,1)S(1)}, u32[]{:S(2)}, u32[]{:S(2)}) collective-permute-start(bf16[1,256,1024]{2,1,0:T(8,128)(2,1)S(1)} %get-tuple-element.115), channel_id=1, source_target_pairs={{0,2},{1,3},{2,0},{3,1},{4,6},{5,7},{6,4},{7,5}} | collective-permute-start | bytes 1572872 | tf_op jit(solution)/shard_map/ppermute | solution.py:325
  1277.9 56.2 %collective-permute-start.13 = (bf16[1,256,1024]{2,1,0:T(8,128)(2,1)S(1)}, bf16[1,256,1024]{2,1,0:T(8,128)(2,1)S(1)}, u32[]{:S(2)}, u32[]{:S(2)}) collective-permute-start(bf16[1,256,1024]{2,1,0:T(8,128)(2,1)S(1)} %get-tuple-element.114), channel_id=1, source_target_pairs={{0,2},{1,3},{2,0},{3,1},{4,6},{5,7},{6,4},{7,5}} | collective-permute-start | bytes 1572872 | tf_op jit(solution)/shard_map/ppermute | solution.py:325
  1328.5 11.6 collective-permute-start.11
  1334.1 7.2 collective-permute-start.14
  (29 other events, 432.0 us)
Sparse Core Ops, SparseCore 0:
  9.8 160.8 all-gather.9
  173.1 84.1 all-gather.7
  259.7 84.1 all-gather.5
  1434.8 44.7 all-reduce.2

commit v2 on v1

--- a/solution.py
+++ b/solution.py
@@ -16,39 +16,53 @@
 GROUP_SIZES = (3, 2, 2, 1)
 
 
-def gather_kernel(scaled, src_ref, rows_ref, table_ref, tok_ref, gate_ref, out_ref):
+def first_gather_kernel(src_ref, rows_ref, table_ref, tok_ref, gate_ref, out_ref, hot_ref):
     @pl.when(pl.program_id(1) * TM < rows_ref[pl.program_id(0)])
     def _():
         n_tok = table_ref.shape[0]
         tok = tok_ref[...]
         lane = lax.broadcasted_iota(jnp.int32, tok.shape, 1).astype(jnp.float32)
         hot = jnp.concatenate([jnp.where(tok == lane + float(j), 1.0, 0.0).astype(jnp.bfloat16) for j in range(0, n_tok, 128)], axis=1)
+        hot_ref[...] = hot
         got = jnp.dot(hot, table_ref[...], preferred_element_type=jnp.float32)
-        if scaled:
-            got = got * gate_ref[:, 0:1]
-        out_ref[...] = got.astype(jnp.bfloat16)
-
-
-def gather_rows(scaled, src_ids, n_rows, table, tok, gate, n_tok):
-    n_src, cap = tok.shape[0], tok.shape[1]
+        out_ref[...] = (got * gate_ref[:, 0:1]).astype(jnp.bfloat16)
+
+
+def next_gather_kernel(src_ref, rows_ref, table_ref, hot_ref, out_ref):
+    @pl.when(pl.program_id(1) * TM < rows_ref[pl.program_id(0)])
+    def _():
+        out_ref[...] = jnp.dot(hot_ref[...], table_ref[...], preferred_element_type=jnp.float32).astype(jnp.bfloat16)
+
+
+def gather_rows(src_ids, n_rows, table, n_tok, cap, hot=None, tok=None, gate=None):
+    n_src = n_rows.shape[0]
     width = table.shape[1]
-    col = pl.BlockSpec((None, TM, 128), lambda k, r, *_: (k, r, 0))
+
+    def at(k, r, src, rows):
+        return (k, jnp.minimum(r, jnp.maximum(lax.div(rows[k] + (TM - 1), TM) - 1, 0)), 0)
+
+    col = pl.BlockSpec((None, TM, 128), at)
+    hot_spec = pl.BlockSpec((None, TM, n_tok), at)
+    row_spec = pl.BlockSpec((None, TM, width), at)
+    table_spec = pl.BlockSpec((n_tok, width), lambda k, r, src, rows: (src[k], 0))
+    row_shape = jax.ShapeDtypeStruct((n_src, cap, width), jnp.bfloat16)
+    first = hot is None
     return pl.pallas_call(
-        functools.partial(gather_kernel, scaled),
-        out_shape=jax.ShapeDtypeStruct((n_src, cap, width), jnp.bfloat16),
+        first_gather_kernel if first else next_gather_kernel,
+        out_shape=(row_shape, jax.ShapeDtypeStruct((n_src, cap, n_tok), jnp.bfloat16)) if first else row_shape,
         grid_spec=pltpu.PrefetchScalarGridSpec(
             num_scalar_prefetch=2,
             grid=(n_src, cap // TM),
-            in_specs=[pl.BlockSpec((n_tok, width), lambda k, r, src, *_: (src[k], 0)), col, col],
-            out_specs=pl.BlockSpec((None, TM, width), lambda k, r, *_: (k, r, 0)),
+            in_specs=[table_spec, col, col] if first else [table_spec, hot_spec],
+            out_specs=[row_spec, hot_spec] if first else row_spec,
         ),
         compiler_params=pltpu.CompilerParams(dimension_semantics=("arbitrary", "arbitrary"), vmem_limit_bytes=40000000),
         cost_estimate=pl.CostEstimate(flops=n_src * cap * n_tok * width, bytes_accessed=n_src * (cap + n_tok) * width * 2, transcendentals=0),
         name="gather_rows",
-    )(src_ids, n_rows, table, tok, gate)
-
-
-def expert_kernel(e0, n_src, n_own, n_chunk, cnt_ref, soff_ref, off_ref, xa_hbm, xb_hbm, dy_hbm, wg_ref, wu_ref, wd_ref, _gg, _gu, _gd, gg_ref, gu_ref, gd_ref, *refs):
+    )(src_ids, n_rows, table, *((tok, gate) if first else (hot,)))
+
+
+def expert_kernel(e0, n_src, n_own, n_chunk, cnt_ref, soff_ref, off_ref, order_ref, xa_hbm, xb_hbm, dy_hbm, wg_ref, wu_ref, wd_ref, _gg, _gu, _gd, gg_ref, gu_ref, gd_ref, *refs):
     out_hbm, refs = refs[:n_own], refs[n_own:]
     xbuf, dobuf, xt, o_acc, dx_acc, gxs, gds, ost, dxst, load_sem, out_sem = refs
     le = pl.program_id(0)
@@ -79,6 +93,23 @@
                     else:
                         cp.wait()
 
+    def outputs(expert, place, start):
+        for s in range(n_own):
+            n = pl.multiple_of(cnt_ref[expert, s], SUB)
+
+            @pl.when(n > 0)
+            def _():
+                src = pl.ds(pl.multiple_of(off_ref[expert, s], SUB), n)
+                copies = (
+                    pltpu.make_async_copy(ost.at[src], out_hbm[s].at[0, place, pl.ds(0, n)], out_sem.at[0]),
+                    pltpu.make_async_copy(dxst.at[src], out_hbm[s].at[1, place, pl.ds(0, n)], out_sem.at[1]),
+                )
+                for cp in copies:
+                    if start:
+                        cp.start()
+                    else:
+                        cp.wait()
+
     own_rows = off_ref[e, n_own]
     tot_rows = off_ref[e, n_src]
     nt_own = lax.div(own_rows + (TM - 1), TM)
@@ -108,6 +139,10 @@
     @pl.when((c == 1) & (le + 1 < n_e))
     def _():
         loads(e + 1, 1 - slot, True)
+
+    @pl.when((c == 2) & (le > 0))
+    def _():
+        outputs(e - 1, le - 1, False)
 
     @pl.when(nt == 0)
     def _():
@@ -168,25 +203,14 @@
             return 0
 
         lax.fori_loop(0, nt_own, cast, 0)
-        for start in (True, False):
-            for s in range(n_own):
-                n = pl.multiple_of(cnt_ref[e, s], SUB)
-
-                @pl.when(n > 0)
-                def _():
-                    src = pl.ds(pl.multiple_of(off_ref[e, s], SUB), n)
-                    copies = (
-                        pltpu.make_async_copy(ost.at[src], out_hbm[s].at[0, le, pl.ds(0, n)], out_sem.at[0]),
-                        pltpu.make_async_copy(dxst.at[src], out_hbm[s].at[1, le, pl.ds(0, n)], out_sem.at[1]),
-                    )
-                    for cp in copies:
-                        if start:
-                            cp.start()
-                        else:
-                            cp.wait()
-
-
-def run_experts(e0, n_e, cnt, soff, off, x_src, dy_src, seg_cap, w_gate, w_up, w_down, prev):
+        outputs(e, le, True)
+
+        @pl.when(le + 1 == n_e)
+        def _():
+            outputs(e, le, False)
+
+
+def run_experts(e0, n_e, cnt, soff, off, order, x_src, dy_src, seg_cap, w_gate, w_up, w_down, prev):
     n_src, cap, width = dy_src.shape
     n_loc = w_gate.shape[0]
     n_own = n_src // 2
@@ -195,8 +219,8 @@
     own_cap = n_own * seg_cap
     bf16 = jnp.bfloat16
     f32 = jnp.float32
-    col_spec = pl.BlockSpec((None, width, CF), lambda i, c, *_: (e0 + i, 0, c))
-    row_spec = pl.BlockSpec((None, CF, width), lambda i, c, *_: (e0 + i, c, 0))
+    col_spec = pl.BlockSpec((None, width, CF), lambda i, c, cnt, soff, off, order: (order[e0 + i], 0, c))
+    row_spec = pl.BlockSpec((None, CF, width), lambda i, c, cnt, soff, off, order: (order[e0 + i], c, 0))
     any_spec = pl.BlockSpec(memory_space=pl.ANY)
     first = prev is None
     if first:
@@ -207,12 +231,12 @@
         jax.ShapeDtypeStruct((n_loc, ff, width), bf16),
     ) + (jax.ShapeDtypeStruct((2, n_e, seg_cap, width), bf16),) * n_own
     rows_est = n_e * cap // 2
-    n_in = 9
+    n_in = 10
     return pl.pallas_call(
         functools.partial(expert_kernel, e0, n_src, n_own, n_chunk),
         out_shape=out_shape,
         grid_spec=pltpu.PrefetchScalarGridSpec(
-            num_scalar_prefetch=3,
+            num_scalar_prefetch=4,
             grid=(n_e, n_chunk),
             in_specs=[any_spec] * 3 + [col_spec, col_spec, row_spec] + [any_spec] * 3,
             out_specs=[col_spec, col_spec, row_spec] + [any_spec] * n_own,
@@ -234,7 +258,7 @@
         compiler_params=pltpu.CompilerParams(dimension_semantics=("arbitrary", "arbitrary"), vmem_limit_bytes=64000000),
         cost_estimate=pl.CostEstimate(flops=2 * 9 * rows_est * width * ff, bytes_accessed=n_e * width * ff * 12, transcendentals=0),
         name="experts",
-    )(cnt, soff, off, *x_src, dy_src, w_gate, w_up, w_down, *prev)
+    )(cnt, soff, off, order, *x_src, dy_src, w_gate, w_up, w_down, *prev)
 
 
 def solution(mesh):
@@ -283,6 +307,7 @@
         slot_gate = slots[:, 1]
         mine = jnp.concatenate([slot_tok, slot_gate, counts.astype(f32), jnp.sum(router_probs, axis=0), jnp.zeros((64,), f32)])
         table = lax.all_gather(mine, all_axes, axis=0, tiled=False)
+        all_counts = table[:, 2 * n_slot:2 * n_slot + n_exp]
         route_stats = jnp.sum(table[:, 2 * n_slot:2 * n_slot + 2 * n_exp], axis=0)
         load_frac = route_stats[:n_exp] / (2 * total_tok)
         aux_loss = AUX_COEF * n_exp * jnp.sum(load_frac * route_stats[n_exp:] / total_tok)
@@ -301,17 +326,33 @@
         off = jnp.concatenate([jnp.zeros((n_loc, 1), jnp.int32), jnp.cumsum(cnt, axis=1)], axis=1)
         n_rows = jnp.sum(cnt, axis=0)
         src_vec = jnp.stack(src_ids).astype(jnp.int32)
-        dy_src = gather_rows(True, src_vec, n_rows, dy_all, tok_col, gate_col, n_tok)
-        xa_all, dy_src = lax.optimization_barrier((xa_all, dy_src))
-        xa_src = gather_rows(False, src_vec, n_rows, xa_all, tok_col, gate_col, n_tok)
+        dy_src, hot = gather_rows(src_vec, n_rows, dy_all, n_tok, owner_rows, tok=tok_col, gate=gate_col)
+        xa_all, hot = lax.optimization_barrier((xa_all, hot))
+        xa_src = gather_rows(src_vec, n_rows, xa_all, n_tok, owner_rows, hot=hot)
         xb_all, xa_src = lax.optimization_barrier((xb_all, xa_src))
-        x_src = (xa_src, gather_rows(False, src_vec, n_rows, xb_all, tok_col, gate_col, n_tok))
+        x_src = (xa_src, gather_rows(src_vec, n_rows, xb_all, n_tok, owner_rows, hot=hot))
+
+        blocks = (all_counts.astype(jnp.int32) + (SUB - 1)) // SUB * SUB
+        own_blocks = jnp.where(d_ix == 0, blocks[:n_ep], blocks[n_ep:])
+        work = 3 * ((jnp.sum(own_blocks, axis=0) + (TM - 1)) // TM) + 6 * ((jnp.sum(blocks, axis=0) + (TM - 1)) // TM)
+        work = work.reshape(n_ep, n_loc)
+        place = jnp.arange(n_loc, dtype=jnp.int32)
+        ahead = (work[:, None, :] > work[:, :, None]) | ((work[:, None, :] == work[:, :, None]) & (place[None, None, :] < place[None, :, None]))
+        rank = jnp.sum(ahead.astype(jnp.int32), axis=2)
+        my_rank = lax.dynamic_index_in_dim(rank, e_ix, 0, keepdims=False)
+        turn = (my_rank[None, :] == place[:, None]).astype(jnp.int32)
+        order = jnp.sum(turn * place[None, :], axis=1)
+
+        def in_order(arr):
+            return jnp.sum(turn[:, :, None] * arr[None], axis=1)
+
+        cnt, soff, off = in_order(cnt), in_order(soff), in_order(off)
 
         prev = None
         backs = [[] for _ in range(n_ep)]
         e0 = 0
         for per in GROUP_SIZES:
-            outs = run_experts(e0, per, cnt, soff, off, x_src, dy_src, capacity, w_gate, w_up, w_down, prev)
+            outs = run_experts(e0, per, cnt, soff, off, order, x_src, dy_src, capacity, w_gate, w_up, w_down, prev)
             prev = outs[:3]
             e0 += per
             for k in range(n_ep):
@@ -328,7 +369,7 @@
         back_rows = jnp.concatenate([b[0] for bk in backs for b in bk], axis=0).reshape(n_slot, width)
         d_back = jnp.concatenate([b[1] for bk in backs for b in bk], axis=0).reshape(n_slot, width)
         owner = dest_rows // owner_rows
-        back_ix = (lax.rem(e_ix - owner + n_ep, n_ep) * owner_rows + lax.rem(dest_rows, owner_rows)).reshape(n_tok, 2)
+        back_ix = (lax.rem(e_ix - owner + n_ep, n_ep) * owner_rows + jnp.sum(one_hot * rank.reshape(1, -1), axis=1) * capacity + lax.rem(dest_rows, capacity)).reshape(n_tok, 2)
 
         def picks(rows):
             return [rows.at[back_ix[:, j]].get(mode="promise_in_bounds").astype(f32) for j in range(2)]
@@ -345,8 +386,9 @@
         d_xnorm = d_xnorm.astype(jnp.bfloat16).astype(f32)
         scaled = d_xnorm * norm_gain
         grad_hidden = (inv_rms * (scaled - x_hat * jnp.mean(scaled * x_hat, axis=-1, keepdims=True)) + dy_f32).astype(jnp.bfloat16)
-        grad_router = lax.psum(jnp.einsum("td,te->de", xn_f32, d_logits), all_axes)
-        grad_gain = lax.psum(jnp.sum(d_xnorm * x_hat, axis=0), all_axes)
+        small = jnp.concatenate([jnp.einsum("td,te->ed", xn_f32, d_logits), jnp.sum(d_xnorm * x_hat, axis=0)[None, :]], axis=0)
+        small = jnp.sum(lax.all_gather(small, all_axes, axis=0, tiled=False), axis=0)
+        grad_router, grad_gain = small[:n_exp].T, small[n_exp]
         return (out_hidden, aux_loss, grad_hidden, grad_gain, grad_router, g_gate, g_up, g_down)
 
     tok_spec = P(all_axes, None)

time: 1500 us -> 1490 us (level)
  blocking collectives: 43.5 us -> 19.3 us
    psum x1 -> x0, blocking collectives: 24.1 us -> none  [local_body(): grad_gain = lax.psum(jnp.sum(d_xnorm * x_hat, axis=0), all_axes)]
    unnamed x89 -> x77, local copies, waits for them, and re-layouts: 50.5 us -> 37.4 us
  transfers between devices with their start and end apart: 19 -> 19, of which waited for: 10 -> 9; matrix products, arithmetic and copies ran while one was open for 8% -> 8% of each run, Pallas kernels for 37% -> 36%
where the time goes in v2:
time: 1490 us; the launch traced here: 1480 us
  Pallas kernels  894 us (60%)
  waiting for transfers between devices  311 us (21%)
  local copies, waits for them, and re-layouts  161 us (11%)
  other arithmetic  52.5 us (4%)
  blocking collectives  19.3 us (1%)
  between operations  16.5 us (1%)
  starting transfers between devices  16.4 us (1%)
    pallas_call x4, Pallas kernels, run_experts(): pl.pallas_call(functools.partial(expert_kernel, e0, n_src, n_own, n_chunk...  696 us
    pallas_call x3, Pallas kernels, gather_rows(): pl.pallas_call(first_gather_kernel if first else next_gather_kernel, out_...  199 us
    ppermute x9, waiting for transfers between devices, local_body(): moved = lax.ppermute(sent, 'ep', ring)  116 us
    all_gather x1, waiting for transfers between devices, local_body(): dy_all = lax.all_gather(grad_out, all_axes, axis=0, tiled=True)  76.8 us
    gather x4, local copies, waits for them, and re-layouts, picks(): rows.at[back_ix[:, j]].get(mode='promise_in_bounds').astype(f32)  75.6 us
    ppermute x3, waiting for transfers between devices, local_body(): lax.ppermute(sent[0], 'ep', ring)  47.4 us
    unnamed x77, local copies, waits for them, and re-layouts  37.4 us
  transfers between devices with their start and end apart: 19, of which 9 were waited for; matrix products, arithmetic and copies ran while one was open for 8% of the time, Pallas kernels for 36%

profile of v2, /device:TPU:0, one launch (start us, length us, event | category | flops | bytes accessed | tf_op | source)
XLA Modules:
  0.0 1480.2 jit_solution(1338515891458998459)
XLA Ops:
  30.1 9.2 reduce-window.6
  43.4 15.3 %scatter_fusion = f32[8192,2]{1,0:T(8,128)} fusion(f32[8192,2]{1,0:T(8,128)} %broadcast_in_dim.12, s32[4096]{0:T(1024)S(1)} %bitcast.211, f32[4096,2]{1,0:T(8,128)S(1)} %copy.89), kind=kCustom, calls=%fused_computation.4 | custom fusion | bytes 114688 | tf_op jit(solution)/shard_map/scatter | solution.py:305
  65.6 19.3 %all-gather.2 = f32[8,1,16512]{2,1,0:T(1,128)S(1)} all-gather(f32[1,1,16512]{2,1,0:T(1,128)S(1)} %reshape.562), channel_id=2, replica_groups=mesh['dp'=2,'ep'=4] {'dp','ep'}, dimensions={0}, use_global_device_ids=true | all-gather | bytes 594432 | tf_op jit(solution)/shard_map/all_gather | solution.py:309
  93.9 76.8 %all-gather.13.cloned.1.call-done.table_ref = bf16[16384,1024]{1,0:T(8,128)(2,1)} async-done(((bf16[2048,1024]{1,0:T(8,128)(2,1)}), bf16[16384,1024]{1,0:T(8,128)(2,1)}) %all-gather.13.cloned.1.call-update) | async-done | bytes 33554448 | tf_op jit(solution)/shard_map/all_gather | solution.py:278
  177.7 82.4 %gather_rows.3 = (bf16[8,2048,1024]{2,1,0:T(8,128)(2,1)}, bf16[8,2048,2048]{2,1,0:T(8,128)(2,1)}) custom-call(s32[8]{0:T(128)S(1)} %stack.106.src_ref, s32[8]{0:T(128)S(1)} %get-tuple-element.87.rows_ref, bf16[16384,1024]{1,0:T(8,128)(2,1)} %all-gather.13.cloned.1.call-done.table_ref, f32[8,2048,128]{2,1,0:T(8,128)S(1)} %broadcast_in_dim.14.tok_ref, ...), custom_call_target="tpu_custom_call" | custom-call | flops 34359738368 | bytes 67108864 | tf_op jit(solution)/shard_map/gather_rows/pallas_call | solution.py:50
  260.1 58.6 %gather_rows.4.xa_hbm = bf16[8,2048,512]{2,1,0:T(8,128)(2,1)} custom-call(s32[8]{0:T(128)S(1)} %stack.106.src_ref, s32[8]{0:T(128)S(1)} %get-tuple-element.87.rows_ref, bf16[16384,512]{1,0:T(8,128)(2,1)} %all-gather.11.cloned.1.call-done.table_ref, bf16[8,2048,2048]{2,1,0:T(8,128)(2,1)} %get-tuple-element.44.hot_ref), custom_call_target="tpu_custom_call" | custom-call | flops 17179869184 | bytes 33554432 | tf_op jit(solution)/shard_map/gather_rows/pallas_call | solution.py:50
  318.7 25.2 %all-gather.9.cloned.1.call-done.table_ref = bf16[16384,512]{1,0:T(8,128)(2,1)} async-done(((bf16[2048,512]{1,0:T(8,128)(2,1)}), bf16[16384,512]{1,0:T(8,128)(2,1)}) %all-gather.9.cloned.1.call-update) | async-done | bytes 16777232 | tf_op jit(solution)/shard_map/all_gather | solution.py:286
  343.9 57.8 %gather_rows.5.xb_hbm = bf16[8,2048,512]{2,1,0:T(8,128)(2,1)} custom-call(s32[8]{0:T(128)S(1)} %stack.106.src_ref, s32[8]{0:T(128)S(1)} %get-tuple-element.87.rows_ref, bf16[16384,512]{1,0:T(8,128)(2,1)} %all-gather.9.cloned.1.call-done.table_ref, bf16[8,2048,2048]{2,1,0:T(8,128)(2,1)} %get-tuple-element.44.hot_ref), custom_call_target="tpu_custom_call" | custom-call | flops 17179869184 | bytes 33554432 | tf_op jit(solution)/shard_map/gather_rows/pallas_call | solution.py:50
  402.3 296.6 %experts.4 = (bf16[8,1024,2816]{2,1,0:T(8,128)(2,1)}, bf16[8,1024,2816]{2,1,0:T(8,128)(2,1)}, bf16[8,2816,1024]{2,1,0:T(8,128)(2,1)}, bf16[2,3,256,1024]{3,2,1,0...) custom-call(s32[8,8]{1,0:T(8,128)} %get-tuple-element.85.cnt_ref, ...), custom_call_target="tpu_custom_call" | custom-call | flops 159450660864 | bytes 103809024 | tf_op jit(solution)/shard_map/experts/pallas_call | solution.py:235
  698.9 168.1 %experts.5 = (bf16[8,1024,2816]{2,1,0:T(8,128)(2,1)}, bf16[8,1024,2816]{2,1,0:T(8,128)(2,1)}, bf16[8,2816,1024]{2,1,0:T(8,128)(2,1)}, bf16[2,2,256,1024]{3,2,1,0...) custom-call(s32[8,8]{1,0:T(8,128)} %get-tuple-element.85.cnt_ref, ...), custom_call_target="tpu_custom_call", output_to_operand_aliasing={{0}: (10, {}), {1}: (11, {}), {2}: (12, {})} | custom-call | flops 106300440576 | bytes 69206016 | tf_op jit(solution)/shard_map/experts/pallas_call | solution.py:235
  867.1 155.4 %experts.6 = (bf16[8,1024,2816]{2,1,0:T(8,128)(2,1)}, bf16[8,1024,2816]{2,1,0:T(8,128)(2,1)}, bf16[8,2816,1024]{2,1,0:T(8,128)(2,1)}, bf16[2,2,256,1024]{3,2,1,0...) custom-call(s32[8,8]{1,0:T(8,128)} %get-tuple-element.85.cnt_ref, ...), custom_call_target="tpu_custom_call", output_to_operand_aliasing={{0}: (10, {}), {1}: (11, {}), {2}: (12, {})} | custom-call | flops 106300440576 | bytes 69206016 | tf_op jit(solution)/shard_map/experts/pallas_call | solution.py:235
  1022.6 75.4 %experts.7 = (bf16[8,1024,2816]{2,1,0:T(8,128)(2,1)}, bf16[8,1024,2816]{2,1,0:T(8,128)(2,1)}, bf16[8,2816,1024]{2,1,0:T(8,128)(2,1)}, bf16[2,1,256,1024]{3,2,1,0...) custom-call(s32[8,8]{1,0:T(8,128)} %get-tuple-element.85.cnt_ref, ...), custom_call_target="tpu_custom_call", output_to_operand_aliasing={{0}: (10, {}), {1}: (11, {}), {2}: (12, {})} | custom-call | flops 53150220288 | bytes 34603008 | tf_op jit(solution)/shard_map/experts/pallas_call | solution.py:235
  1113.9 24.0 %collective-permute-done.12 = bf16[1,256,1024]{2,1,0:T(8,128)(2,1)S(1)} collective-permute-done((bf16[1,256,1024]{2,1,0:T(8,128)(2,1)S(1)}, bf16[1,256,1024]{2,1,0:T(8,128)(2,1)S(1)}, u32[]{:S(2)}, u32[]{:S(2)}) %collective-permute-start.12) | collective-permute-done | bytes 524320 | tf_op jit(solution)/shard_map/ppermute | solution.py:366
  1163.9 94.0 %collective-permute-done.5 = bf16[2,2,256,1024]{3,2,1,0:T(8,128)(2,1)S(1)} collective-permute-done((bf16[2,2,256,1024]{3,2,1,0:T(8,128)(2,1)S(1)}, bf16[2,2,256,1024]{3,2,1,0:T(8,128)(2,1)S(1)}, u32[]{:S(2)}, u32[]{:S(2)}) %collective-permute-start.5) | collective-permute-done | bytes 2097184 | tf_op jit(solution)/shard_map/ppermute | solution.py:364
  1257.9 22.5 %collective-permute-done.6 = bf16[2,2,256,1024]{3,2,1,0:T(8,128)(2,1)S(1)} collective-permute-done((bf16[2,2,256,1024]{3,2,1,0:T(8,128)(2,1)S(1)}, bf16[2,2,256,1024]{3,2,1,0:T(8,128)(2,1)S(1)}, u32[]{:S(2)}, u32[]{:S(2)}) %collective-permute-start.6) | collective-permute-done | bytes 2097184 | tf_op jit(solution)/shard_map/ppermute | solution.py:364
  1283.5 47.4 %collective-permute-done.7 = bf16[1,256,1024]{2,1,0:T(8,128)(2,1)S(1)} collective-permute-done((bf16[1,256,1024]{2,1,0:T(8,128)(2,1)S(1)}, bf16[1,256,1024]{2,1,0:T(8,128)(2,1)S(1)}, u32[]{:S(2)}, u32[]{:S(2)}) %collective-permute-start.7) | collective-permute-done | bytes 524320 | tf_op jit(solution)/shard_map/ppermute | solution.py:366
  1344.3 18.9 %gather_fusion.1 = bf16[2048,1024]{1,0:T(8,128)(2,1)} fusion(bf16[8192,1024]{1,0:T(8,128)(2,1)} %bitcast.53, s32[2048]{0:T(1024)S(1)} %copy-done.14), kind=kCustom, calls=%fused_computation.1 | custom fusion | bytes 8396800 | tf_op jit(solution)/shard_map/gather | solution.py:375
  1363.2 18.9 %gather_fusion = bf16[2048,1024]{1,0:T(8,128)(2,1)} fusion(bf16[8192,1024]{1,0:T(8,128)(2,1)} %bitcast.53, s32[2048]{0:T(1024)S(1)} %copy-done.15), kind=kCustom, calls=%fused_computation | custom fusion | bytes 8396800 | tf_op jit(solution)/shard_map/gather | solution.py:375
  1382.1 10.3 fusion.12
  1398.1 18.9 %gather_fusion.2 = bf16[2048,1024]{1,0:T(8,128)(2,1)} fusion(bf16[8192,1024]{1,0:T(8,128)(2,1)} %bitcast.75, s32[2048]{0:T(1024)S(1)} %copy-done.15), kind=kCustom, calls=%fused_computation.2 | custom fusion | bytes 8396800 | tf_op jit(solution)/shard_map/gather | solution.py:375
  1417.1 18.9 %gather_fusion.3 = bf16[2048,1024]{1,0:T(8,128)(2,1)} fusion(bf16[8192,1024]{1,0:T(8,128)(2,1)} %bitcast.75, s32[2048]{0:T(1024)S(1)} %copy-done.14), kind=kCustom, calls=%fused_computation.3 | custom fusion | bytes 8396800 | tf_op jit(solution)/shard_map/gather | solution.py:375
  1436.0 11.0 fusion.9
  1448.3 7.3 fusion.14
  1455.7 14.0 all-gather.15.cloned.1.call-done
  (206 shorter events, 117.4 us)
Async XLA Ops:
  7.2 163.5 %all-gather.13.cloned.1.call-start = ((), (), s32[]{:S(2)}) async-start(), calls=%async_computation.2 | async-start | bytes 37748736 | tf_op jit(solution)/shard_map/all_gather | solution.py:278
  7.9 252.2 %all-gather.11.cloned.1.call-start = ((), (), s32[]{:S(2)}) async-start(), calls=%async_computation.1 | async-start | bytes 18874368 | tf_op jit(solution)/shard_map/all_gather | solution.py:285
  19.3 324.6 %all-gather.9.cloned.1.call-start = ((), (), s32[]{:S(2)}) async-start(), calls=%async_computation | async-start | bytes 18874368 | tf_op jit(solution)/shard_map/all_gather | solution.py:286
  20.1 1449.6 %all-gather.15.cloned.1.call-start = ((), (), s32[]{:S(2)}) async-start(), calls=%async_computation.3 | async-start | bytes 1474560 | tf_op jit(solution)/shard_map/all_gather | solution.py:390
  698.9 445.3 %collective-permute-start = (bf16[2,3,256,1024]{3,2,1,0:T(8,128)(2,1)}, bf16[2,3,256,1024]{3,2,1,0:T(8,128)(2,1)}, u32[]{:S(2)}, u32[]{:S(2)}) collective-permute-start(bf16[2,3,256,1024]{3,2,1,0:T(8,128)(2,1)} %get-tuple-element.61), channel_id=1, source_target_pairs={{0,1},{1,2},{2,3},{3,0},{4,5},{5,6},{6,7},{7,4}} | collective-permute-start | bytes 9437192 | tf_op jit(solution)/shard_map/ppermute | solution.py:364
  867.0 271.0 %collective-permute-start.1 = (bf16[2,2,256,1024]{3,2,1,0:T(8,128)(2,1)}, bf16[2,2,256,1024]{3,2,1,0:T(8,128)(2,1)}, u32[]{:S(2)}, u32[]{:S(2)}) collective-permute-start(bf16[2,2,256,1024]{3,2,1,0:T(8,128)(2,1)} %get-tuple-element.62), channel_id=1, source_target_pairs={{0,1},{1,2},{2,3},{3,0},{4,5},{5,6},{6,7},{7,4}} | collective-permute-start | bytes 6291464 | tf_op jit(solution)/shard_map/ppermute | solution.py:364
  867.0 290.2 %collective-permute-start.4 = (bf16[2,3,256,1024]{3,2,1,0:T(8,128)(2,1)}, bf16[2,3,256,1024]{3,2,1,0:T(8,128)(2,1)}, u32[]{:S(2)}, u32[]{:S(2)}) collective-permute-start(bf16[2,3,256,1024]{3,2,1,0:T(8,128)(2,1)} %get-tuple-element.65), channel_id=1, source_target_pairs={{0,2},{1,3},{2,0},{3,1},{4,6},{5,7},{6,4},{7,5}} | collective-permute-start | bytes 9437192 | tf_op jit(solution)/shard_map/ppermute | solution.py:364
  1022.5 83.7 %copy-start.20 = (f32[64]{0:T(128)S(1)}, f32[64]{0:T(128)}, u32[]{:S(2)}) copy-start(f32[64]{0:T(128)} %slice_reduce_fusion.3) | copy-start | bytes 772
  1022.5 84.3 %copy-start.27 = (bf16[2,2,256,1024]{3,2,1,0:T(8,128)(2,1)S(1)}, bf16[2,2,256,1024]{3,2,1,0:T(8,128)(2,1)}, u32[]{:S(2)}) copy-start(bf16[2,2,256,1024]{3,2,1,0:T(8,128)(2,1)} %get-tuple-element.63) | copy-start | bytes 6291460
  1098.0 40.0 %copy-start.25 = (bf16[2,2,256,1024]{3,2,1,0:T(8,128)(2,1)S(1)}, bf16[2,2,256,1024]{3,2,1,0:T(8,128)(2,1)}, u32[]{:S(2)}) copy-start(bf16[2,2,256,1024]{3,2,1,0:T(8,128)(2,1)} %get-tuple-element.66) | copy-start | bytes 6291460
  1098.1 46.1 %copy-start.26 = (bf16[2,2,256,1024]{3,2,1,0:T(8,128)(2,1)S(1)}, bf16[2,2,256,1024]{3,2,1,0:T(8,128)(2,1)}, u32[]{:S(2)}) copy-start(bf16[2,2,256,1024]{3,2,1,0:T(8,128)(2,1)} %get-tuple-element.67) | copy-start | bytes 6291460
  1098.1 46.2 %copy-start.5 = (bf16[2,2,256,1024]{3,2,1,0:T(8,128)(2,1)S(1)}, bf16[2,2,256,1024]{3,2,1,0:T(8,128)(2,1)}, u32[]{:S(2)}) copy-start(bf16[2,2,256,1024]{3,2,1,0:T(8,128)(2,1)} %get-tuple-element.56) | copy-start | bytes 6291460
  1099.5 11.7 collective-permute-start.3
  1106.9 47.4 %collective-permute-start.2 = (bf16[2,2,256,1024]{3,2,1,0:T(8,128)(2,1)S(1)}, bf16[2,2,256,1024]{3,2,1,0:T(8,128)(2,1)S(1)}, u32[]{:S(2)}, u32[]{:S(2)}) collective-permute-start(bf16[2,2,256,1024]{3,2,1,0:T(8,128)(2,1)S(1)} %copy-done.27), channel_id=1, source_target_pairs={{0,1},{1,2},{2,3},{3,0},{4,5},{5,6},{6,7},{7,4}} | collective-permute-start | bytes 6291464 | tf_op jit(solution)/shard_map/ppermute | solution.py:364
  1111.2 26.8 %collective-permute-start.12 = (bf16[1,256,1024]{2,1,0:T(8,128)(2,1)S(1)}, bf16[1,256,1024]{2,1,0:T(8,128)(2,1)S(1)}, u32[]{:S(2)}, u32[]{:S(2)}) collective-permute-start(bf16[1,256,1024]{2,1,0:T(8,128)(2,1)S(1)} %get-tuple-element.124), channel_id=1, source_target_pairs={{0,1},{1,2},{2,3},{3,0},{4,5},{5,6},{6,7},{7,4}} | collective-permute-start | bytes 1572872 | tf_op jit(solution)/shard_map/ppermute | solution.py:366
  1138.0 199.4 %collective-permute-start.8 = (bf16[2,3,256,1024]{3,2,1,0:T(8,128)(2,1)S(1)}, bf16[2,3,256,1024]{3,2,1,0:T(8,128)(2,1)S(1)}, u32[]{:S(2)}, u32[]{:S(2)}) collective-permute-start(bf16[2,3,256,1024]{3,2,1,0:T(8,128)(2,1)S(1)} %copy-done.22), channel_id=1, source_target_pairs={{0,3},{1,0},{2,1},{3,2},{4,7},{5,4},{6,5},{7,6}} | collective-permute-start | bytes 9437192 | tf_op jit(solution)/shard_map/ppermute | solution.py:364
  1138.1 119.8 %collective-permute-start.5 = (bf16[2,2,256,1024]{3,2,1,0:T(8,128)(2,1)S(1)}, bf16[2,2,256,1024]{3,2,1,0:T(8,128)(2,1)S(1)}, u32[]{:S(2)}, u32[]{:S(2)}) collective-permute-start(bf16[2,2,256,1024]{3,2,1,0:T(8,128)(2,1)S(1)} %copy-done.25), channel_id=1, source_target_pairs={{0,2},{1,3},{2,0},{3,1},{4,6},{5,7},{6,4},{7,5}} | collective-permute-start | bytes 6291464 | tf_op jit(solution)/shard_map/ppermute | solution.py:364
  1144.2 136.2 %collective-permute-start.6 = (bf16[2,2,256,1024]{3,2,1,0:T(8,128)(2,1)S(1)}, bf16[2,2,256,1024]{3,2,1,0:T(8,128)(2,1)S(1)}, u32[]{:S(2)}, u32[]{:S(2)}) collective-permute-start(bf16[2,2,256,1024]{3,2,1,0:T(8,128)(2,1)S(1)} %copy-done.26), channel_id=1, source_target_pairs={{0,2},{1,3},{2,0},{3,1},{4,6},{5,7},{6,4},{7,5}} | collective-permute-start | bytes 6291464 | tf_op jit(solution)/shard_map/ppermute | solution.py:364
  1154.2 185.3 %collective-permute-start.9 = (bf16[2,2,256,1024]{3,2,1,0:T(8,128)(2,1)S(1)}, bf16[2,2,256,1024]{3,2,1,0:T(8,128)(2,1)S(1)}, u32[]{:S(2)}, u32[]{:S(2)}) collective-permute-start(bf16[2,2,256,1024]{3,2,1,0:T(8,128)(2,1)S(1)} %copy-done.23), channel_id=1, source_target_pairs={{0,3},{1,0},{2,1},{3,2},{4,7},{5,4},{6,5},{7,6}} | collective-permute-start | bytes 6291464 | tf_op jit(solution)/shard_map/ppermute | solution.py:364
  1157.3 183.8 %collective-permute-start.10 = (bf16[2,2,256,1024]{3,2,1,0:T(8,128)(2,1)S(1)}, bf16[2,2,256,1024]{3,2,1,0:T(8,128)(2,1)S(1)}, u32[]{:S(2)}, u32[]{:S(2)}) collective-permute-start(bf16[2,2,256,1024]{3,2,1,0:T(8,128)(2,1)S(1)} %copy-done.24), channel_id=1, source_target_pairs={{0,3},{1,0},{2,1},{3,2},{4,7},{5,4},{6,5},{7,6}} | collective-permute-start | bytes 6291464 | tf_op jit(solution)/shard_map/ppermute | solution.py:364
  1257.9 73.0 %collective-permute-start.7 = (bf16[1,256,1024]{2,1,0:T(8,128)(2,1)S(1)}, bf16[1,256,1024]{2,1,0:T(8,128)(2,1)S(1)}, u32[]{:S(2)}, u32[]{:S(2)}) collective-permute-start(bf16[1,256,1024]{2,1,0:T(8,128)(2,1)S(1)} %get-tuple-element.123), channel_id=1, source_target_pairs={{0,2},{1,3},{2,0},{3,1},{4,6},{5,7},{6,4},{7,5}} | collective-permute-start | bytes 1572872 | tf_op jit(solution)/shard_map/ppermute | solution.py:366
  1280.3 56.2 %collective-permute-start.13 = (bf16[1,256,1024]{2,1,0:T(8,128)(2,1)S(1)}, bf16[1,256,1024]{2,1,0:T(8,128)(2,1)S(1)}, u32[]{:S(2)}, u32[]{:S(2)}) collective-permute-start(bf16[1,256,1024]{2,1,0:T(8,128)(2,1)S(1)} %get-tuple-element.122), channel_id=1, source_target_pairs={{0,2},{1,3},{2,0},{3,1},{4,6},{5,7},{6,4},{7,5}} | collective-permute-start | bytes 1572872 | tf_op jit(solution)/shard_map/ppermute | solution.py:366
  1330.9 11.7 collective-permute-start.11
  1336.5 6.7 collective-permute-start.14
  (23 other events, 347.0 us)
Sparse Core Ops, SparseCore 0:
  9.8 160.8 all-gather.12
  173.1 84.1 all-gather.10
  259.7 84.1 all-gather.8
  1447.8 21.7 all-gather.14
